TPU v7x, 8 devices: a whole 2x2x1 slice. The times are simulated.
8 devices in a mesh: fsdp: 8 (over z, y, x, core).
Axes of the slice: x: 2, y: 2, z: 1, core: 2. Of those that a mesh axis runs over, the one named last changes fastest.
Arguments:
- tok_ids: int32 [8, 4096], P('fsdp')
- tok_labels: int32 [8, 4096], P('fsdp')
- embed: bfloat16 [32128, 768], P('fsdp')
- w_gate: bfloat16 [768, 3072], P('fsdp')
- w_up: bfloat16 [768, 3072], P('fsdp')
- w_down: bfloat16 [3072, 768], P('fsdp')
- gain_mlp: float32 [768], replicated
- gain_final: float32 [768], replicated
Outputs:
- output 1: float32 [], replicated
- output 2: float32 [32128, 768], P('fsdp')
- output 3: float32 [768, 3072], P('fsdp')
- output 4: float32 [768, 3072], P('fsdp')
- output 5: float32 [3072, 768], P('fsdp')
All inputs are finite; a program needn't handle non-finite values.
Results may differ from a plain program's by a relative error of at most 0.00906315.
Values are sent between devices in bfloat16 or wider.
A program may use at most 1 GiB of HBM per device.

v0:
```python
import math
import jax
import jax.numpy as jnp
from jax import lax
from jax.sharding import PartitionSpec as P

NORM_EPS = 1e-6


def dot_plain(left_mat, right_mat):
    return lax.dot_general(left_mat, right_mat, (((1,), (0,)), ((), ())), preferred_element_type=jnp.float32)


def dot_last(left_mat, right_mat):
    return lax.dot_general(left_mat, right_mat, (((1,), (1,)), ((), ())), preferred_element_type=jnp.float32)


def dot_first(left_mat, right_mat):
    return lax.dot_general(left_mat, right_mat, (((0,), (0,)), ((), ())), preferred_element_type=jnp.float32)


def rms_apply(values, gain_vec):
    inv_rms = lax.rsqrt(jnp.mean(values * values, axis=-1, keepdims=True) + NORM_EPS)
    return (values * inv_rms * gain_vec).astype(jnp.bfloat16), inv_rms


def rms_backward(values, inv_rms, gain_vec, grad_out):
    scaled = grad_out * gain_vec
    return inv_rms * scaled - values * (inv_rms ** 3) * jnp.mean(scaled * values, axis=-1, keepdims=True)


def mlp_forward(x_emb, w_gate, w_up, w_down, gain_mlp, gain_final):
    normed, inv_first = rms_apply(x_emb, gain_mlp)
    gate = dot_plain(normed, w_gate).astype(jnp.bfloat16)
    up_val = dot_plain(normed, w_up).astype(jnp.bfloat16)
    hidden_act = (jax.nn.silu(gate.astype(jnp.float32)) * up_val.astype(jnp.float32)).astype(jnp.bfloat16)
    mlp_out = dot_plain(hidden_act, w_down).astype(jnp.bfloat16)
    hid32 = (x_emb + mlp_out.astype(jnp.float32)).astype(jnp.bfloat16).astype(jnp.float32)
    hid_norm, inv_final = rms_apply(hid32, gain_final)
    return hid_norm, (x_emb, inv_first, normed, gate, up_val, hidden_act, hid32, inv_final)


def mlp_backward(d_hid, saved, w_gate, w_up, w_down, gain_mlp, gain_final):
    x_emb, inv_first, normed, gate, up_val, hidden_act, hid32, inv_final = saved
    d_hidden = rms_backward(hid32, inv_final, gain_final, d_hid)
    d_mlp = d_hidden.astype(jnp.bfloat16)
    d_down = dot_first(hidden_act, d_mlp)
    d_act = dot_last(d_mlp, w_down)
    gate32 = gate.astype(jnp.float32)
    gate_sig = jax.nn.sigmoid(gate32)
    d_gate_pre = (d_act * up_val.astype(jnp.float32) * gate_sig * (1.0 + gate32 * (1.0 - gate_sig))).astype(jnp.bfloat16)
    d_up_pre = (d_act * gate32 * gate_sig).astype(jnp.bfloat16)
    d_gate = dot_first(normed, d_gate_pre)
    d_up = dot_first(normed, d_up_pre)
    d_normed = dot_last(d_gate_pre, w_gate) + dot_last(d_up_pre, w_up)
    d_x = (d_hidden + rms_backward(x_emb, inv_first, gain_mlp, d_normed)).astype(jnp.bfloat16)
    return d_x, d_gate, d_up, d_down


def head_forward(hid_norm, emb_chunks, lab_flat):
    chunk_rows = emb_chunks.shape[1]
    tok_count = hid_norm.shape[0]
    col_ids = jnp.arange(chunk_rows, dtype=jnp.int32)

    def chunk_step(carry, chunk_in):
        run_max, run_sum, lab_logit = carry
        chunk_emb, chunk_idx = chunk_in
        logits = dot_last(hid_norm, chunk_emb)
        label_hit = (lab_flat - chunk_idx * chunk_rows)[:, None] == col_ids[None, :]
        new_max = jnp.maximum(run_max, jnp.max(logits, axis=1))
        run_sum = run_sum * jnp.exp(run_max - new_max) + jnp.sum(jnp.exp(logits - new_max[:, None]), axis=1)
        lab_logit = lab_logit + jnp.sum(jnp.where(label_hit, logits, 0.0), axis=1)
        return (new_max, run_sum, lab_logit), None

    zero_tok = jnp.zeros((tok_count,), jnp.float32)
    start = (jnp.full((tok_count,), -jnp.inf, jnp.float32), zero_tok, zero_tok)
    chunk_ids = jnp.arange(emb_chunks.shape[0], dtype=jnp.int32)
    (run_max, run_sum, lab_logit), unused = lax.scan(chunk_step, start, (emb_chunks, chunk_ids))
    return run_max + jnp.log(run_sum), lab_logit


def head_backward(hid_norm, emb_chunks, lab_flat, log_norm, inv_count):
    chunk_rows = emb_chunks.shape[1]
    col_ids = jnp.arange(chunk_rows, dtype=jnp.int32)

    def chunk_step(d_hid, chunk_in):
        chunk_emb, chunk_idx = chunk_in
        logits = dot_last(hid_norm, chunk_emb)
        label_hit = (lab_flat - chunk_idx * chunk_rows)[:, None] == col_ids[None, :]
        prob_mat = jnp.exp(logits - log_norm[:, None])
        grad_logits = ((prob_mat - label_hit.astype(jnp.float32)) * inv_count).astype(jnp.bfloat16)
        return d_hid + dot_plain(grad_logits, chunk_emb), dot_first(grad_logits, hid_norm)

    chunk_ids = jnp.arange(emb_chunks.shape[0], dtype=jnp.int32)
    d_hid, d_head = lax.scan(chunk_step, jnp.zeros(hid_norm.shape, jnp.float32), (emb_chunks, chunk_ids))
    return d_hid, d_head.reshape(-1, hid_norm.shape[1])


def solution(mesh):
    group = mesh.shape['fsdp']

    def local_step(ids_blk, lab_blk, emb_shard, gate_shard, up_shard, down_shard, gain_mlp, gain_final):
        embed_full = lax.all_gather(emb_shard, 'fsdp', tiled=True)
        w_gate = lax.all_gather(gate_shard, 'fsdp', tiled=True)
        w_up = lax.all_gather(up_shard, 'fsdp', tiled=True)
        w_down = lax.all_gather(down_shard, 'fsdp', tiled=True)
        ids_flat = ids_blk.reshape(-1)
        lab_flat = lab_blk.reshape(-1)
        model_dim = embed_full.shape[1]
        emb_scale = math.sqrt(model_dim)
        inv_count = 1.0 / (ids_flat.shape[0] * group)
        x_emb = jnp.take(embed_full, ids_flat, axis=0).astype(jnp.float32) * emb_scale
        hid_norm, saved = mlp_forward(x_emb, w_gate, w_up, w_down, gain_mlp, gain_final)
        emb_chunks = embed_full.reshape(group, -1, model_dim)
        log_norm, lab_logit = head_forward(hid_norm, emb_chunks, lab_flat)
        loss = lax.psum(jnp.sum(log_norm - lab_logit), 'fsdp') * inv_count
        d_hid, d_head = head_backward(hid_norm, emb_chunks, lab_flat, log_norm, inv_count)
        d_x, d_gate, d_up, d_down = mlp_backward(d_hid, saved, w_gate, w_up, w_down, gain_mlp, gain_final)
        d_full = d_head.at[ids_flat].add(d_x.astype(jnp.float32) * emb_scale)
        d_embed = lax.psum_scatter(d_full, 'fsdp', scatter_dimension=0, tiled=True)
        d_gate = lax.psum_scatter(d_gate, 'fsdp', scatter_dimension=0, tiled=True)
        d_up = lax.psum_scatter(d_up, 'fsdp', scatter_dimension=0, tiled=True)
        d_down = lax.psum_scatter(d_down, 'fsdp', scatter_dimension=0, tiled=True)
        return loss, d_embed, d_gate, d_up, d_down

    shard_spec = P('fsdp', None)
    return jax.shard_map(local_step, mesh=mesh, in_specs=(shard_spec, shard_spec, shard_spec, shard_spec, shard_spec, shard_spec, P(), P()), out_specs=(P(), shard_spec, shard_spec, shard_spec, shard_spec), check_vma=False)
```

profile of v0, /device:TPU:0, one launch (start us, length us, event | category | flops | bytes accessed | tf_op | source)
XLA Modules:
  0.0 2693.7 jit_solution(5899000218577954439)
XLA Ops:
  12.1 223.0 %all-gather.5.cloned.1.call-done = bf16[32128,768]{1,0:T(8,128)(2,1)} async-done(((bf16[4016,768]{1,0:T(8,128)(2,1)}), bf16[32128,768]{1,0:T(8,128)(2,1)}) %all-gather.5.cloned.1.call-update) | async-done | bytes 49348624 | tf_op jit(solution)/shard_map/all_gather | solution.py:103
  235.2 70.9 %gather_fusion = bf16[4096,768]{1,0:T(8,128)(2,1)} fusion(bf16[32128,768]{1,0:T(8,128)(2,1)} %all-gather.5.cloned.1.call-done, s32[4096]{0:T(1024)S(1)} %broadcast_clamp_fusion.1), kind=kCustom, calls=%fused_computation | custom fusion | bytes 12599296 | tf_op jit(solution)/shard_map/jit(_take)/gather | solution.py:112
  348.8 40.4 %fusion.21 = (bf16[4096,3072]{1,0:T(8,128)(2,1)}, bf16[4096,3072]{1,0:T(8,128)(2,1)}) fusion(bf16[4096,3072]{1,0:T(8,128)(2,1)} %convolution_convert_fusion.1, bf16[768,3072]{1,0:T(8,128)(2,1)} %all-gather.9.cloned.1.call-done, f32[768]{0:T(1024)S(1)} %copy-done.22, f32[4096]{0:T(1024)S(1)} %get-tuple-element.258, bf16[4096,768]{0,1:T(8,128)(2,1)} %copy.22, ...), kind=kOutput, calls=%fused_computation.39 | convolution fusion | flops 19456327680 | bytes 86531072 | tf_op jit(solution)/shard_map/dot_general | solution.py:11
  435.8 464.8 %while.28 = (s32[]{:T(128)}, f32[4096]{0:T(1024)S(1)}, f32[4096]{0:T(1024)S(1)}, f32[4096]{0:T(1024)S(1)}, bf16[8,4016,768]{2,1,0:T(8,128)(2,1)}, /*index=5*/bf1...) while((s32[]{:T(128)}, f32[4096]{0:T(1024)S(1)}, ...), condition=%wide.region_6.7_spmd.clone, body=%wide.region_2.0_spmd.clone.sunk | while | flops 25365213184 | bytes 144384656 | solution.py:78
  435.9 35.5 %fusion.98 = (f32[4096]{0:T(1024)S(1)}, f32[4016,4096]{1,0:T(8,128)}) fusion(bf16[4096,768]{1,0:T(8,128)(2,1)} %get-tuple-element.405, bf16[8,4016,768]{2,1,0:T(8,128)(2,1)} %get-tuple-element.404, s32[]{:T(128)} %get-tuple-element.389), kind=kOutput, calls=%fused_computation.103.clone.1 | convolution fusion | flops 25282932736 | bytes 78275072 | tf_op jit(solution)/shard_map/while/body/eval_jaxpr/dot_general | solution.py:15
  901.3 905.1 %while.29 = (s32[]{:T(128)}, f32[4096,768]{1,0:T(8,128)}, f32[8,4016,768]{2,1,0:T(8,128)}, bf16[8,4016,768]{2,1,0:T(8,128)(2,1)}, bf16[4096,768]{1,0:T(8,128)(2,...) while((s32[]{:T(128)}, f32[4096,768]{1,0:T(8,128)}, ...), condition=%wide.region_10.11_spmd.clone, body=%wide.region_9.10_spmd.clone.sunk | while | flops 75904450560 | bytes 161187472 | solution.py:95
  902.7 43.3 %fusion.106 = bf16[4096,4016]{0,1:T(8,128)(2,1)} fusion(bf16[4096,768]{1,0:T(8,128)(2,1)} %get-tuple-element.437, s32[4096]{0:T(1024)S(1)} %broadcast_subtract_fusion.5, f32[4096]{0:T(1024)S(1)} %get-tuple-element.438, bf16[8,4016,768]{2,1,0:T(8,128)(2,1)} %get-tuple-element.436, s32[]{:T(128)} %get-tuple-element.422), kind=kOutput, calls=%fused_computation.23.clone.1 | convolution fusion | flops 25365184512 | bytes 45392384 | tf_op jit(solution)/shard_map/while/body/eval_jaxpr/dot_general | solution.py:15
  1015.0 43.4 %fusion.106 = bf16[4096,4016]{0,1:T(8,128)(2,1)} fusion(bf16[4096,768]{1,0:T(8,128)(2,1)} %get-tuple-element.437, s32[4096]{0:T(1024)S(1)} %broadcast_subtract_fusion.5, f32[4096]{0:T(1024)S(1)} %get-tuple-element.438, bf16[8,4016,768]{2,1,0:T(8,128)(2,1)} %get-tuple-element.436, s32[]{:T(128)} %get-tuple-element.422), kind=kOutput, calls=%fused_computation.23.clone.1 | convolution fusion | flops 25365184512 | bytes 45392384 | tf_op jit(solution)/shard_map/while/body/eval_jaxpr/dot_general | solution.py:15
  1091.1 35.8 %select_add_fusion.5 = f32[4096,768]{1,0:T(8,128)} fusion(f32[4096,768]{1,0:T(8,128)} %get-tuple-element.423, bf16[4096,4016]{0,1:T(8,128)(2,1)} %fusion.106, pred[]{:T(512)S(6)} %compare.10, bf16[8,4016,768]{2,1,0:T(8,128)(2,1)} %get-tuple-element.436, s32[]{:T(128)} %get-tuple-element.422), kind=kOutput, calls=%fused_computation.24.clone.1 | convolution fusion | flops 25272778752 | bytes 64233984 | tf_op jit(solution)/shard_map/while/body/eval_jaxpr/dot_general | solution.py:11
  1128.2 43.4 %fusion.106 = bf16[4096,4016]{0,1:T(8,128)(2,1)} fusion(bf16[4096,768]{1,0:T(8,128)(2,1)} %get-tuple-element.437, s32[4096]{0:T(1024)S(1)} %broadcast_subtract_fusion.5, f32[4096]{0:T(1024)S(1)} %get-tuple-element.438, bf16[8,4016,768]{2,1,0:T(8,128)(2,1)} %get-tuple-element.436, s32[]{:T(128)} %get-tuple-element.422), kind=kOutput, calls=%fused_computation.23.clone.1 | convolution fusion | flops 25365184512 | bytes 45392384 | tf_op jit(solution)/shard_map/while/body/eval_jaxpr/dot_general | solution.py:15
  1204.3 35.8 %select_add_fusion.5 = f32[4096,768]{1,0:T(8,128)} fusion(f32[4096,768]{1,0:T(8,128)} %get-tuple-element.423, bf16[4096,4016]{0,1:T(8,128)(2,1)} %fusion.106, pred[]{:T(512)S(6)} %compare.10, bf16[8,4016,768]{2,1,0:T(8,128)(2,1)} %get-tuple-element.436, s32[]{:T(128)} %get-tuple-element.422), kind=kOutput, calls=%fused_computation.24.clone.1 | convolution fusion | flops 25272778752 | bytes 64233984 | tf_op jit(solution)/shard_map/while/body/eval_jaxpr/dot_general | solution.py:11
  1241.3 43.4 %fusion.106 = bf16[4096,4016]{0,1:T(8,128)(2,1)} fusion(bf16[4096,768]{1,0:T(8,128)(2,1)} %get-tuple-element.437, s32[4096]{0:T(1024)S(1)} %broadcast_subtract_fusion.5, f32[4096]{0:T(1024)S(1)} %get-tuple-element.438, bf16[8,4016,768]{2,1,0:T(8,128)(2,1)} %get-tuple-element.436, s32[]{:T(128)} %get-tuple-element.422), kind=kOutput, calls=%fused_computation.23.clone.1 | convolution fusion | flops 25365184512 | bytes 45392384 | tf_op jit(solution)/shard_map/while/body/eval_jaxpr/dot_general | solution.py:15
  1317.4 35.8 %select_add_fusion.5 = f32[4096,768]{1,0:T(8,128)} fusion(f32[4096,768]{1,0:T(8,128)} %get-tuple-element.423, bf16[4096,4016]{0,1:T(8,128)(2,1)} %fusion.106, pred[]{:T(512)S(6)} %compare.10, bf16[8,4016,768]{2,1,0:T(8,128)(2,1)} %get-tuple-element.436, s32[]{:T(128)} %get-tuple-element.422), kind=kOutput, calls=%fused_computation.24.clone.1 | convolution fusion | flops 25272778752 | bytes 64233984 | tf_op jit(solution)/shard_map/while/body/eval_jaxpr/dot_general | solution.py:11
  1354.5 43.4 %fusion.106 = bf16[4096,4016]{0,1:T(8,128)(2,1)} fusion(bf16[4096,768]{1,0:T(8,128)(2,1)} %get-tuple-element.437, s32[4096]{0:T(1024)S(1)} %broadcast_subtract_fusion.5, f32[4096]{0:T(1024)S(1)} %get-tuple-element.438, bf16[8,4016,768]{2,1,0:T(8,128)(2,1)} %get-tuple-element.436, s32[]{:T(128)} %get-tuple-element.422), kind=kOutput, calls=%fused_computation.23.clone.1 | convolution fusion | flops 25365184512 | bytes 45392384 | tf_op jit(solution)/shard_map/while/body/eval_jaxpr/dot_general | solution.py:15
  1430.6 35.8 %select_add_fusion.5 = f32[4096,768]{1,0:T(8,128)} fusion(f32[4096,768]{1,0:T(8,128)} %get-tuple-element.423, bf16[4096,4016]{0,1:T(8,128)(2,1)} %fusion.106, pred[]{:T(512)S(6)} %compare.10, bf16[8,4016,768]{2,1,0:T(8,128)(2,1)} %get-tuple-element.436, s32[]{:T(128)} %get-tuple-element.422), kind=kOutput, calls=%fused_computation.24.clone.1 | convolution fusion | flops 25272778752 | bytes 64233984 | tf_op jit(solution)/shard_map/while/body/eval_jaxpr/dot_general | solution.py:11
  1467.6 43.4 %fusion.106 = bf16[4096,4016]{0,1:T(8,128)(2,1)} fusion(bf16[4096,768]{1,0:T(8,128)(2,1)} %get-tuple-element.437, s32[4096]{0:T(1024)S(1)} %broadcast_subtract_fusion.5, f32[4096]{0:T(1024)S(1)} %get-tuple-element.438, bf16[8,4016,768]{2,1,0:T(8,128)(2,1)} %get-tuple-element.436, s32[]{:T(128)} %get-tuple-element.422), kind=kOutput, calls=%fused_computation.23.clone.1 | convolution fusion | flops 25365184512 | bytes 45392384 | tf_op jit(solution)/shard_map/while/body/eval_jaxpr/dot_general | solution.py:15
  1543.8 35.8 %select_add_fusion.5 = f32[4096,768]{1,0:T(8,128)} fusion(f32[4096,768]{1,0:T(8,128)} %get-tuple-element.423, bf16[4096,4016]{0,1:T(8,128)(2,1)} %fusion.106, pred[]{:T(512)S(6)} %compare.10, bf16[8,4016,768]{2,1,0:T(8,128)(2,1)} %get-tuple-element.436, s32[]{:T(128)} %get-tuple-element.422), kind=kOutput, calls=%fused_computation.24.clone.1 | convolution fusion | flops 25272778752 | bytes 64233984 | tf_op jit(solution)/shard_map/while/body/eval_jaxpr/dot_general | solution.py:11
  1580.8 43.4 %fusion.106 = bf16[4096,4016]{0,1:T(8,128)(2,1)} fusion(bf16[4096,768]{1,0:T(8,128)(2,1)} %get-tuple-element.437, s32[4096]{0:T(1024)S(1)} %broadcast_subtract_fusion.5, f32[4096]{0:T(1024)S(1)} %get-tuple-element.438, bf16[8,4016,768]{2,1,0:T(8,128)(2,1)} %get-tuple-element.436, s32[]{:T(128)} %get-tuple-element.422), kind=kOutput, calls=%fused_computation.23.clone.1 | convolution fusion | flops 25365184512 | bytes 45392384 | tf_op jit(solution)/shard_map/while/body/eval_jaxpr/dot_general | solution.py:15
  1657.0 35.8 %select_add_fusion.5 = f32[4096,768]{1,0:T(8,128)} fusion(f32[4096,768]{1,0:T(8,128)} %get-tuple-element.423, bf16[4096,4016]{0,1:T(8,128)(2,1)} %fusion.106, pred[]{:T(512)S(6)} %compare.10, bf16[8,4016,768]{2,1,0:T(8,128)(2,1)} %get-tuple-element.436, s32[]{:T(128)} %get-tuple-element.422), kind=kOutput, calls=%fused_computation.24.clone.1 | convolution fusion | flops 25272778752 | bytes 64233984 | tf_op jit(solution)/shard_map/while/body/eval_jaxpr/dot_general | solution.py:11
  1694.1 43.4 %fusion.106 = bf16[4096,4016]{0,1:T(8,128)(2,1)} fusion(bf16[4096,768]{1,0:T(8,128)(2,1)} %get-tuple-element.437, s32[4096]{0:T(1024)S(1)} %broadcast_subtract_fusion.5, f32[4096]{0:T(1024)S(1)} %get-tuple-element.438, bf16[8,4016,768]{2,1,0:T(8,128)(2,1)} %get-tuple-element.436, s32[]{:T(128)} %get-tuple-element.422), kind=kOutput, calls=%fused_computation.23.clone.1 | convolution fusion | flops 25365184512 | bytes 45392384 | tf_op jit(solution)/shard_map/while/body/eval_jaxpr/dot_general | solution.py:15
  1770.2 35.8 %select_add_fusion.5 = f32[4096,768]{1,0:T(8,128)} fusion(f32[4096,768]{1,0:T(8,128)} %get-tuple-element.423, bf16[4096,4016]{0,1:T(8,128)(2,1)} %fusion.106, pred[]{:T(512)S(6)} %compare.10, bf16[8,4016,768]{2,1,0:T(8,128)(2,1)} %get-tuple-element.436, s32[]{:T(128)} %get-tuple-element.422), kind=kOutput, calls=%fused_computation.24.clone.1 | convolution fusion | flops 25272778752 | bytes 64233984 | tf_op jit(solution)/shard_map/while/body/eval_jaxpr/dot_general | solution.py:11
  1858.5 50.8 %fusion.30 = (bf16[4096,3072]{1,0:T(8,128)(2,1)}, bf16[4096,3072]{1,0:T(8,128)(2,1)}) fusion(bf16[4096,3072]{1,0:T(8,128)(2,1)} %convolution_convert_fusion.1, bf16[4096,3072]{1,0:T(8,128)(2,1)} %get-tuple-element.263, bf16[3072,768]{1,0:T(8,128)(2,1)} %all-gather.11.cloned.1.call-done, f32[4096]{0:T(1024)S(1)} %broadcast_multiply_fusion.2, ...), kind=kOutput, calls=%fused_computation.48 | convolution fusion | flops 19538116608 | bytes 124308480 | tf_op jit(solution)/shard_map/dot_general | solution.py:15
  2051.8 124.1 %scatter_custom_fusion = f32[32128,768]{1,0:T(8,128)} fusion(f32[32128,768]{1,0:T(8,128)} %bitcast.5, s32[4096]{0:T(1024)S(1)} %get-tuple-element.213, f32[4096,768]{1,0:T(8,128)} %copy.26, s32[4096]{0:T(1024)S(1)} %broadcast_clamp_fusion), kind=kCustom, calls=%fused_computation.76 | custom fusion | flops 3145728 | bytes 98697216 | tf_op jit(solution)/shard_map/scatter-add | solution.py:119
  2199.2 486.1 %reduce-scatter.13.cloned.1.call-done = f32[4016,768]{1,0:T(8,128)} async-done(((f32[32128,768]{1,0:T(8,128)}), f32[4016,768]{1,0:T(8,128)}) %reduce-scatter.13.cloned.1.call-update) | async-done | bytes 12337168
  (196 shorter events, 1037.2 us)
Async XLA Ops:
  7.2 228.0 %all-gather.5.cloned.1.call-start = ((), (), s32[]{:S(2)}) async-start(), calls=%async_computation.4 | async-start | bytes 55517184 | tf_op jit(solution)/shard_map/all_gather | solution.py:103
  7.9 312.3 %all-gather.7.cloned.1.call-start = ((), (), s32[]{:S(2)}) async-start(), calls=%async_computation.5 | async-start | bytes 5308416 | tf_op jit(solution)/shard_map/all_gather | solution.py:104
  8.6 340.2 %all-gather.9.cloned.1.call-start = ((), (), s32[]{:S(2)}) async-start(), calls=%async_computation.6 | async-start | bytes 5308416 | tf_op jit(solution)/shard_map/all_gather | solution.py:105
  9.4 379.9 %all-gather.11.cloned.1.call-start = ((), (), s32[]{:S(2)}) async-start(), calls=%async_computation.7 | async-start | bytes 5308416 | tf_op jit(solution)/shard_map/all_gather | solution.py:106
  10.0 2189.2 %reduce-scatter.11.cloned.1.call-start = ((), (), s32[]{:S(2)}) async-start(), calls=%async_computation.10 | async-start | bytes 10616832 | tf_op jit(solution)/shard_map/reduce_scatter | solution.py:123
  12.1 377.1 %copy-start.18 = (pred[4096]{0:T(1024)(128)(4,1)}, pred[4096]{0:T(1024)(128)(4,1)S(1)}, u32[]{:S(2)}) copy-start(pred[4096]{0:T(1024)(128)(4,1)S(1)} %compare_and_fusion) | copy-start | bytes 12292
  320.2 28.6 %copy-start.20 = (f32[4096]{0:T(1024)}, f32[4096]{0:T(1024)S(1)}, u32[]{:S(2)}) copy-start(f32[4096]{0:T(1024)S(1)} %get-tuple-element.258) | copy-start | bytes 49156
  389.3 29.8 %copy-start.15 = (f32[768]{0:T(1024)S(1)}, f32[768]{0:T(1024)}, u32[]{:S(2)}) copy-start(f32[768]{0:T(1024)} %param.19) | copy-start | bytes 9220
  1828.2 30.3 %copy-start.11 = (f32[4096]{0:T(1024)}, f32[4096]{0:T(1024)S(1)}, u32[]{:S(2)}) copy-start(f32[4096]{0:T(1024)S(1)} %broadcast_multiply_fusion.2) | copy-start | bytes 49156
  1858.4 340.7 %reduce-scatter.7.cloned.1.call-start = ((), (), s32[]{:S(2)}) async-start(), calls=%async_computation.8 | async-start | bytes 10616832 | tf_op jit(solution)/shard_map/reduce_scatter | solution.py:121
  1858.5 50.8 %copy-start.19 = (pred[4096]{0:T(1024)(128)(4,1)S(1)}, pred[4096]{0:T(1024)(128)(4,1)}, u32[]{:S(2)}) copy-start(pred[4096]{0:T(1024)(128)(4,1)} %copy-done.18) | copy-start | bytes 12292
  1858.5 50.8 %copy-start.21 = (f32[4096]{0:T(1024)S(1)}, f32[4096]{0:T(1024)}, u32[]{:S(2)}) copy-start(f32[4096]{0:T(1024)} %copy-done.20) | copy-start | bytes 49156
  1858.5 50.8 %copy-start.23 = (f32[768]{0:T(1024)S(1)}, f32[768]{0:T(1024)}, u32[]{:S(2)}) copy-start(f32[768]{0:T(1024)} %param.18) | copy-start | bytes 9220
  1936.7 262.5 %reduce-scatter.9.cloned.1.call-start = ((), (), s32[]{:S(2)}) async-start(), calls=%async_computation.9 | async-start | bytes 10616832 | tf_op jit(solution)/shard_map/reduce_scatter | solution.py:122
  1964.0 31.7 %slice-start.3 = ((s8[6291456]{0:T(1024)(128)(4,1)}), s8[2097152]{0:T(1024)(128)(4,1)S(1)}, s32[]{:S(2)}) async-start(s8[6291456]{0:T(1024)(128)(4,1)} %bitcast.83), calls=%async_computation.15 | async-start | bytes 4194304
  1964.0 721.2 %reduce-scatter.13.cloned.1.call-start = ((), (), s32[]{:S(2)}) async-start(), calls=%async_computation.11 | async-start | bytes 111034368
  1969.3 54.9 %slice-start = ((s8[12582912]{0:T(1024)(128)(4,1)}), s8[4194304]{0:T(1024)(128)(4,1)S(1)}, s32[]{:S(2)}) async-start(s8[12582912]{0:T(1024)(128)(4,1)} %bitcast.81), calls=%async_computation.12 | async-start | bytes 8388608
  1969.3 54.9 %slice-start.1 = ((s8[12582912]{0:T(1024)(128)(4,1)}), s8[4194304]{0:T(1024)(128)(4,1)S(1)}, s32[]{:S(2)}) async-start(s8[12582912]{0:T(1024)(128)(4,1)} %bitcast.81), calls=%async_computation.13 | async-start | bytes 8388608
  1995.8 28.4 %slice-start.2 = ((s8[12582912]{0:T(1024)(128)(4,1)}), s8[4194304]{0:T(1024)(128)(4,1)S(1)}, s32[]{:S(2)}) async-start(s8[12582912]{0:T(1024)(128)(4,1)} %bitcast.81), calls=%async_computation.14 | async-start | bytes 8388608
  1995.8 28.4 %copy-start.6 = (f32[4096]{0:T(1024)S(1)}, f32[4096]{0:T(1024)}, u32[]{:S(2)}) copy-start(f32[4096]{0:T(1024)} %copy-done.4) | copy-start | bytes 49156
  1995.8 28.4 %copy-start.10 = (f32[4096]{0:T(1024)S(1)}, f32[4096]{0:T(1024)}, u32[]{:S(2)}) copy-start(f32[4096]{0:T(1024)} %get-tuple-element.260) | copy-start | bytes 49156
  1995.8 28.4 %copy-start.12 = (f32[4096]{0:T(1024)S(1)}, f32[4096]{0:T(1024)}, u32[]{:S(2)}) copy-start(f32[4096]{0:T(1024)} %copy-done.11) | copy-start | bytes 49156
  1995.8 28.4 %copy-start.13 = (f32[4096]{0:T(1024)S(1)}, f32[4096]{0:T(1024)}, u32[]{:S(2)}) copy-start(f32[4096]{0:T(1024)} %get-tuple-element.257) | copy-start | bytes 49156
  1995.8 28.4 %copy-start.14 = (f32[4096]{0:T(1024)S(1)}, f32[4096]{0:T(1024)}, u32[]{:S(2)}) copy-start(f32[4096]{0:T(1024)} %get-tuple-element.259) | copy-start | bytes 49156
  (13 other events, 195.8 us)
Sparse Core Ops, SparseCore 0:
  9.8 225.3 all-gather.4
  237.0 32.9 all-gather.6
  271.8 32.9 all-gather.8
  306.4 32.9 all-gather.10
  1858.6 67.4 reduce-scatter.10
  1936.8 67.4 reduce-scatter.6
  2008.3 67.4 reduce-scatter.8
  2176.1 509.1 reduce-scatter.12
where the time goes:
time: 2700 us; the launch traced here: 2690 us
  matrix products  1470 us (54%)
  waiting for transfers between devices  712 us (26%)
  other arithmetic  341 us (13%)
  local copies, waits for them, and re-layouts  124 us (5%)
    dot_general x19, matrix products, dot_last(): lax.dot_general(left_mat, right_mat, (((1,), (1,)), ((), ())), preferred_...  736 us
    unnamed x9, waiting for transfers between devices  489 us
    dot_general x11, matrix products, dot_plain(): lax.dot_general(left_mat, right_mat, (((1,), (0,)), ((), ())), preferred_...  383 us
    dot_general x11, matrix products, dot_first(): lax.dot_general(left_mat, right_mat, (((0,), (0,)), ((), ())), preferred_...  347 us
    all_gather x1, waiting for transfers between devices, local_step(): embed_full = lax.all_gather(emb_shard, 'fsdp', tiled=True)  223 us
    reduce_sum x8, other arithmetic, chunk_step(): lab_logit = lab_logit + jnp.sum(jnp.where(label_hit, logits, 0.0), axis=1)  171 us
    scatter-add x3, other arithmetic, local_step(): d_full = d_head.at[ids_flat].add(d_x.astype(jnp.float32) * emb_scale)  129 us
    gather x2, local copies, waits for them, and re-layouts, local_step(): jnp.take(embed_full, ids_flat, axis=0).astype(jnp.float32) * emb_scale  79.6 us
  transfers between devices with their start and end apart: 8, of which 2 were waited for; matrix products, arithmetic and copies ran while one was open for 18% of the time, Pallas kernels for 0%

commit v1 on v0

v1 whole, which is shorter than its diff:
```python
import functools
import math
import jax
import jax.numpy as jnp
from jax import lax
from jax.experimental import pallas as pl
from jax.experimental.pallas import tpu as pltpu
from jax.sharding import PartitionSpec as P

NORM_EPS = 1e-6


def dot_plain(left_mat, right_mat):
    return lax.dot_general(left_mat, right_mat, (((1,), (0,)), ((), ())), preferred_element_type=jnp.float32)


def dot_last(left_mat, right_mat):
    return lax.dot_general(left_mat, right_mat, (((1,), (1,)), ((), ())), preferred_element_type=jnp.float32)


def dot_first(left_mat, right_mat):
    return lax.dot_general(left_mat, right_mat, (((0,), (0,)), ((), ())), preferred_element_type=jnp.float32)


def rms_apply(values, gain_vec):
    inv_rms = lax.rsqrt(jnp.mean(values * values, axis=-1, keepdims=True) + NORM_EPS)
    return (values * inv_rms * gain_vec).astype(jnp.bfloat16), inv_rms


def rms_backward(values, inv_rms, gain_vec, grad_out):
    scaled = grad_out * gain_vec
    return inv_rms * scaled - values * (inv_rms ** 3) * jnp.mean(scaled * values, axis=-1, keepdims=True)


def mlp_forward(x_emb, w_gate, w_up, w_down, gain_mlp, gain_final):
    normed, inv_first = rms_apply(x_emb, gain_mlp)
    gate = dot_plain(normed, w_gate).astype(jnp.bfloat16)
    up_val = dot_plain(normed, w_up).astype(jnp.bfloat16)
    hidden_act = (jax.nn.silu(gate.astype(jnp.float32)) * up_val.astype(jnp.float32)).astype(jnp.bfloat16)
    mlp_out = dot_plain(hidden_act, w_down).astype(jnp.bfloat16)
    hid32 = (x_emb + mlp_out.astype(jnp.float32)).astype(jnp.bfloat16).astype(jnp.float32)
    hid_norm, inv_final = rms_apply(hid32, gain_final)
    return hid_norm, (x_emb, inv_first, normed, gate, up_val, hidden_act, hid32, inv_final)


def mlp_backward(d_hid, saved, w_gate, w_up, w_down, gain_mlp, gain_final):
    x_emb, inv_first, normed, gate, up_val, hidden_act, hid32, inv_final = saved
    d_hidden = rms_backward(hid32, inv_final, gain_final, d_hid)
    d_mlp = d_hidden.astype(jnp.bfloat16)
    d_down = dot_first(hidden_act, d_mlp)
    d_act = dot_last(d_mlp, w_down)
    gate32 = gate.astype(jnp.float32)
    gate_sig = jax.nn.sigmoid(gate32)
    d_gate_pre = (d_act * up_val.astype(jnp.float32) * gate_sig * (1.0 + gate32 * (1.0 - gate_sig))).astype(jnp.bfloat16)
    d_up_pre = (d_act * gate32 * gate_sig).astype(jnp.bfloat16)
    d_gate = dot_first(normed, d_gate_pre)
    d_up = dot_first(normed, d_up_pre)
    d_normed = dot_last(d_gate_pre, w_gate) + dot_last(d_up_pre, w_up)
    d_x = (d_hidden + rms_backward(x_emb, inv_first, gain_mlp, d_normed)).astype(jnp.bfloat16)
    return d_x, d_gate, d_up, d_down


VM = 64 * 1024 * 1024 - 128 * 1024


def nn(a, b):
    return lax.dot_general(a, b, (((1,), (0,)), ((), ())), preferred_element_type=jnp.float32)


def fwd_kernel(emb_ref, hnt_ref, lse_ref, et_ref, max_ref, sum_ref, top_ref, part_ref, *, n_own, n_blk, rows, tail, tok_tile):
    own, blk = pl.program_id(0), pl.program_id(1)
    tok = hnt_ref.shape[1]
    n_tile = tok // tok_tile

    def logits(emb, cols):
        return nn(emb, hnt_ref[:, cols]).reshape(emb.shape[0] // 8, 8, tok_tile)

    def redo(count):
        emb = emb_ref[0, :count, :]

        def tile(i, carry):
            cols = pl.ds(pl.multiple_of(i * tok_tile, tok_tile), tok_tile)
            z = logits(emb, cols)
            old = max_ref[:, cols]
            new = jnp.maximum(old, jnp.max(z, axis=0))
            max_ref[:, cols] = new
            sum_ref[:, cols] = sum_ref[:, cols] * jnp.exp(old - new) + jnp.sum(jnp.exp(z - new[None]), axis=0)
            return carry

        lax.fori_loop(0, n_tile, tile, 0)

    def run(count):
        emb = emb_ref[0, :count, :]
        et_ref[0, :, :count] = emb.T
        for i in range(n_tile):
            cols = slice(i * tok_tile, (i + 1) * tok_tile)
            z = logits(emb, cols)
            shift = max_ref[:, cols]
            top_ref[:, cols] = jnp.max(z, axis=0) - shift
            part_ref[:, cols] = jnp.sum(jnp.exp(z - shift[None]), axis=0)
        grown = jnp.max(top_ref[...]) > 40.0

        @pl.when(grown)
        def _():
            redo(count)

        @pl.when(jnp.logical_not(grown))
        def _():
            sum_ref[...] += part_ref[...]

    @pl.when((own == 0) & (blk == 0))
    def _():
        max_ref[...] = jnp.full(max_ref.shape, -jnp.inf, jnp.float32)
        sum_ref[...] = jnp.zeros(sum_ref.shape, jnp.float32)
        et_ref[0] = emb_ref[0].T
        redo(rows)

    @pl.when((blk < n_blk - 1) & ((own > 0) | (blk > 0)))
    def _():
        run(rows)

    @pl.when(blk == n_blk - 1)
    def _():
        run(tail)

    @pl.when((own == n_own - 1) & (blk == n_blk - 1))
    def _():
        top = jnp.max(max_ref[...], axis=0, keepdims=True)
        total = jnp.sum(sum_ref[...] * jnp.exp(max_ref[...] - top), axis=0, keepdims=True)
        lse_ref[...] = top + jnp.log(total)


def head_fwd(emb3, hnt, rows=512, tok_tile=1024):
    n_own, per, dim = emb3.shape
    tok = hnt.shape[1]
    n_blk = pl.cdiv(per, rows)
    tail = per - (n_blk - 1) * rows
    return pl.pallas_call(
        functools.partial(fwd_kernel, n_own=n_own, n_blk=n_blk, rows=rows, tail=tail, tok_tile=tok_tile),
        grid=(n_own, n_blk),
        in_specs=[pl.BlockSpec((1, rows, dim), lambda o, b: (o, b, 0)),
                  pl.BlockSpec((dim, tok), lambda o, b: (0, 0))],
        out_specs=[pl.BlockSpec((1, tok), lambda o, b: (0, 0)),
                   pl.BlockSpec((1, dim, rows), lambda o, b: (o, 0, b))],
        out_shape=[jax.ShapeDtypeStruct((1, tok), jnp.float32),
                   jax.ShapeDtypeStruct((n_own, dim, per), jnp.bfloat16)],
        scratch_shapes=[pltpu.VMEM((8, tok), jnp.float32)] * 4,
        compiler_params=pltpu.CompilerParams(dimension_semantics=("arbitrary", "arbitrary"), vmem_limit_bytes=VM),
        cost_estimate=pl.CostEstimate(flops=2 * tok * n_own * per * dim, bytes_accessed=4 * n_own * per * dim, transcendentals=tok * n_own * per),
    )(emb3, hnt)


def bwd_kernel(*refs, first, rows, tok_tile, sub, n_own, per, chunk, block, inv_count):
    if first:
        hn_hbm, hnt_hbm, lse_ref, lab_ref, emb_ref, et_ref, de_ref, zy_ref, dhn_hbm = refs[:9]
        dhn_src = None
        rest = refs[9:]
    else:
        hn_hbm, hnt_hbm, lse_ref, lab_ref, emb_ref, et_ref, dhn_src, de_ref, zy_ref, dhn_hbm = refs[:10]
        rest = refs[10:]
    hn_ref, hnt_ref, dhn_ref, hn_sem, hnt_sem, in_sem, out_sem = rest
    own = pl.program_id(0)
    tok, dim = hn_ref.shape
    step = tok_tile * sub
    n_step = tok // step

    def copies(i):
        cols = pl.ds(pl.multiple_of(i * step, step), step)
        out = [pltpu.make_async_copy(hn_hbm.at[cols, :], hn_ref.at[cols, :], hn_sem.at[i]),
               pltpu.make_async_copy(hnt_hbm.at[:, cols], hnt_ref.at[:, cols], hnt_sem.at[i])]
        if not first:
            out.append(pltpu.make_async_copy(dhn_src.at[:, cols], dhn_ref.at[:, cols], in_sem.at[i]))
        return out

    def out_copy(i):
        cols = pl.ds(pl.multiple_of(i * step, step), step)
        return pltpu.make_async_copy(dhn_ref.at[:, cols], dhn_hbm.at[:, cols], out_sem.at[i])

    @pl.when(own == 0)
    def _():
        for i in range(n_step):
            for c in copies(i):
                c.start()
        zy_ref[...] = jnp.zeros(zy_ref.shape, jnp.float32)
        if first:
            dhn_ref[...] = jnp.zeros(dhn_ref.shape, jnp.float32)

    de_ref[...] = jnp.zeros(de_ref.shape, jnp.float32)
    base = own * per + chunk * block
    emb = emb_ref[0, :rows, :]
    emb_t = et_ref[0, :, :rows]

    def tile(i, carry):
        @pl.when(own == 0)
        def _():
            for c in copies(i):
                c.wait()

        row_ids = lax.broadcasted_iota(jnp.int32, (rows, tok_tile), 0)
        work = []
        for s in range(sub):
            cols = pl.ds(pl.multiple_of(i * step + s * tok_tile, tok_tile), tok_tile)
            work.append((cols, nn(emb, hnt_ref[:, cols])))
        grads = []
        for cols, z in work:
            hit = row_ids == (lab_ref[:, cols] - base)
            prob = jnp.exp(z - lse_ref[:, cols])
            grad = (jnp.where(hit, prob - 1.0, prob) * inv_count).astype(jnp.bfloat16)
            zy_ref[:, cols] += jnp.sum(jnp.where(hit, z, 0.0).reshape(rows // 8, 8, tok_tile), axis=0)
            grads.append((cols, grad))
        for cols, grad in grads:
            dhn_ref[:, cols] += nn(emb_t, grad)
        big = grads[0][1] if sub == 1 else jnp.concatenate([g for _, g in grads], axis=1)
        cols = pl.ds(pl.multiple_of(i * step, step), step)
        de_ref[0] += nn(big, hn_ref[cols, :])

        @pl.when(own == n_own - 1)
        def _():
            out_copy(i).start()
        return carry

    lax.fori_loop(0, n_step, tile, 0)

    @pl.when(own == n_own - 1)
    def _():
        for i in range(n_step):
            out_copy(i).wait()


def head_bwd(hn, hnt, lse, lab, emb3, et3, dhn, chunk, block=512, tok_tile=512, sub=2, inv_count=1.0 / 32768):
    n_own, per, dim = emb3.shape
    tok = hn.shape[0]
    rows = min(block, per - chunk * block)
    first = dhn is None
    n_step = tok // (tok_tile * sub)
    anyspec = pl.BlockSpec(memory_space=pl.ANY)
    row = pl.BlockSpec((1, tok), lambda o: (0, 0))
    ins = [hn, hnt, lse, lab, emb3, et3] + ([] if first else [dhn])
    return pl.pallas_call(
        functools.partial(bwd_kernel, first=first, rows=rows, tok_tile=tok_tile, sub=sub, n_own=n_own, per=per, chunk=chunk, block=block, inv_count=inv_count),
        grid=(n_own,),
        in_specs=[anyspec, anyspec, row, row,
                  pl.BlockSpec((1, block, dim), lambda o: (o, chunk, 0)),
                  pl.BlockSpec((1, dim, block), lambda o: (o, 0, chunk))] + ([] if first else [anyspec]),
        out_specs=[pl.BlockSpec((1, rows, dim), lambda o: (o, 0, 0)), pl.BlockSpec((8, tok), lambda o: (0, 0)), anyspec],
        out_shape=[jax.ShapeDtypeStruct((n_own, rows, dim), jnp.float32), jax.ShapeDtypeStruct((8, tok), jnp.float32),
                   jax.ShapeDtypeStruct((dim, tok), jnp.float32)],
        scratch_shapes=[pltpu.VMEM((tok, dim), jnp.bfloat16), pltpu.VMEM((dim, tok), jnp.bfloat16), pltpu.VMEM((dim, tok), jnp.float32)]
        + [pltpu.SemaphoreType.DMA((n_step,))] * 4,
        input_output_aliases={} if first else {6: 2},
        compiler_params=pltpu.CompilerParams(dimension_semantics=("arbitrary",), vmem_limit_bytes=VM),
        cost_estimate=pl.CostEstimate(flops=6 * tok * n_own * rows * dim, bytes_accessed=50 * 1024 * 1024, transcendentals=tok * n_own * rows),
    )(*ins)


def scatter_kernel(meta_ref, live_ref, ids_ref, dx_hbm, base_ref, out_ref, buf_ref, sem, *, rows, toks, scale):
    blk = pl.program_id(0)
    n_live = meta_ref[0]

    def fetch(j, slot):
        start = pl.multiple_of(live_ref[j] * toks, toks)
        return pltpu.make_async_copy(dx_hbm.at[pl.ds(start, toks), :], buf_ref.at[slot], sem.at[slot])

    @pl.when(n_live > 0)
    def _():
        fetch(0, 0).start()

    out_ref[...] = jnp.zeros(out_ref.shape, jnp.float32)
    row_ids = lax.broadcasted_iota(jnp.int32, (rows, toks), 0) + (blk * rows + meta_ref[1])

    def body(j, carry):
        slot = lax.rem(j, 2)

        @pl.when(j + 1 < n_live)
        def _():
            fetch(j + 1, 1 - slot).start()

        fetch(j, slot).wait()
        cols = pl.ds(pl.multiple_of(live_ref[j] * toks, toks), toks)
        hot = jnp.where(row_ids == ids_ref[:, cols], 1.0, 0.0).astype(jnp.bfloat16)
        out_ref[...] += nn(hot, buf_ref[slot])
        return carry

    lax.fori_loop(0, n_live, body, 0)
    out_ref[...] = base_ref[...] + out_ref[...] * scale


def scatter_rows(ids, d_x, base, first_row, scale, rows=1024, toks=256):
    per, dim = base.shape
    n_blk = ids.shape[0] // toks
    live = jnp.any(((ids >= first_row) & (ids < first_row + per)).reshape(n_blk, toks), axis=1)
    order = jnp.argsort(jnp.logical_not(live)).astype(jnp.int32)
    meta = jnp.stack([jnp.sum(live.astype(jnp.int32)), first_row])
    return pl.pallas_call(
        functools.partial(scatter_kernel, rows=rows, toks=toks, scale=scale),
        grid_spec=pltpu.PrefetchScalarGridSpec(
            num_scalar_prefetch=2, grid=(pl.cdiv(per, rows),),
            in_specs=[pl.BlockSpec((1, ids.shape[0]), lambda b, *_: (0, 0)), pl.BlockSpec(memory_space=pl.ANY),
                      pl.BlockSpec((rows, dim), lambda b, *_: (b, 0))],
            out_specs=pl.BlockSpec((rows, dim), lambda b, *_: (b, 0)),
            scratch_shapes=[pltpu.VMEM((2, toks, dim), d_x.dtype), pltpu.SemaphoreType.DMA((2,))]),
        out_shape=jax.ShapeDtypeStruct((per, dim), jnp.float32),
        compiler_params=pltpu.CompilerParams(dimension_semantics=("arbitrary",), vmem_limit_bytes=VM),
        cost_estimate=pl.CostEstimate(flops=2 * per * 8192 * dim, bytes_accessed=8 * per * dim, transcendentals=0),
    )(meta, order, ids.reshape(1, -1), d_x, base)


def solution(mesh):
    group = mesh.shape['fsdp']

    def local_step(ids_blk, lab_blk, emb_shard, gate_shard, up_shard, down_shard, gain_mlp, gain_final):
        me = lax.axis_index('fsdp')
        per, model_dim = emb_shard.shape
        emb_scale = math.sqrt(model_dim)
        ids_flat, lab_flat = lax.sort((ids_blk.reshape(-1), lab_blk.reshape(-1)), num_keys=1)
        n_tok = ids_flat.shape[0]
        inv_count = 1.0 / (n_tok * group)
        embed_full = lax.all_gather(emb_shard, 'fsdp', tiled=True)
        w_gate = lax.all_gather(gate_shard, 'fsdp', tiled=True)
        w_up = lax.all_gather(up_shard, 'fsdp', tiled=True)
        w_down = lax.all_gather(down_shard, 'fsdp', tiled=True)

        ids_all = lax.all_gather(ids_flat, 'fsdp', tiled=True)

        x_emb = jnp.take(embed_full, ids_flat, axis=0, indices_are_sorted=True).astype(jnp.float32) * emb_scale
        hid_norm, saved = mlp_forward(x_emb, w_gate, w_up, w_down, gain_mlp, gain_final)
        hid_t = hid_norm.T
        emb3 = embed_full.reshape(group, per, model_dim)
        log_norm, emb_t = head_fwd(emb3, hid_t)
        labels = lab_flat.reshape(1, -1)
        block = 512
        d_hid_t, lab_logit, d_rows = None, 0.0, []
        for chunk in range(pl.cdiv(per, block)):
            d_emb, lab_part, d_hid_t = head_bwd(hid_norm, hid_t, log_norm, labels, emb3, emb_t, d_hid_t, chunk, block=block, tok_tile=1024, sub=1, inv_count=inv_count)
            d_rows.append(lax.psum_scatter(d_emb, 'fsdp', scatter_dimension=0, tiled=True)[0])
            lab_logit = lab_logit + lab_part
        loss = lax.psum(jnp.sum(log_norm[0] - jnp.sum(lab_logit, axis=0)), 'fsdp') * inv_count

        d_x, d_gate, d_up, d_down = mlp_backward(d_hid_t.T, saved, w_gate, w_up, w_down, gain_mlp, gain_final)
        d_gate = lax.psum_scatter(d_gate, 'fsdp', scatter_dimension=0, tiled=True)
        d_up = lax.psum_scatter(d_up, 'fsdp', scatter_dimension=0, tiled=True)
        d_down = lax.psum_scatter(d_down, 'fsdp', scatter_dimension=0, tiled=True)
        d_x_all = lax.all_gather(d_x, 'fsdp', tiled=True)
        d_embed = scatter_rows(ids_all, d_x_all, jnp.concatenate(d_rows, axis=0), me * per, emb_scale)
        return loss, d_embed, d_gate, d_up, d_down

    shard_spec = P('fsdp', None)
    return jax.shard_map(local_step, mesh=mesh, in_specs=(shard_spec, shard_spec, shard_spec, shard_spec, shard_spec, shard_spec, P(), P()), out_specs=(P(), shard_spec, shard_spec, shard_spec, shard_spec), check_vma=False)
```

time: 2700 us -> 2410 us (0.89)
  Pallas kernels: 0 us -> 1450 us
  matrix products: 1470 us -> 289 us
  other arithmetic: 341 us -> 52.2 us
  waiting for transfers between devices: 712 us -> 440 us
    pallas_call x0 -> x10, Pallas kernels: none -> 1450 us  [the longest x8 791 us: head_bwd(): pl.pallas_call(functools.partial(bwd_kernel, first=first, rows=rows, tok_...]
    dot_general x19 -> x3, matrix products: 736 us -> 108 us  [dot_last(): lax.dot_general(left_mat, right_mat, (((1,), (1,)), ((), ())), preferred_...]
    unnamed x9 -> x16, waiting for transfers between devices: 489 us -> 2.78 us
    dot_general x11 -> x3, matrix products: 383 us -> 90.6 us  [dot_plain(): lax.dot_general(left_mat, right_mat, (((1,), (0,)), ((), ())), preferred_...]
    dot_general x11 -> x3, matrix products: 347 us -> 90.6 us  [dot_first(): lax.dot_general(left_mat, right_mat, (((0,), (0,)), ((), ())), preferred_...]
    reduce_sum x9 -> x3, other arithmetic: 171 us -> 1.34 us  [the longest x1 0.67 us: scatter_rows(): meta = jnp.stack([jnp.sum(live.astype(jnp.int32)), first_row])]
    scatter-add x3 -> x0, other arithmetic: 129 us -> none  [local_step(): d_full = d_head.at[ids_flat].add(d_x.astype(jnp.float32) * emb_scale)]
    all_gather x0 -> x1, waiting for transfers between devices: none -> 75.5 us  [local_step(): d_x_all = lax.all_gather(d_x, 'fsdp', tiled=True)]
  transfers between devices with their start and end apart: 8 -> 16, of which waited for: 2 -> 5; matrix products, arithmetic and copies ran while one was open for 18% -> 17% of each run, Pallas kernels for 0% -> 32%
where the time goes in v1:
time: 2410 us; the launch traced here: 2390 us
  Pallas kernels  1450 us (60%)
  waiting for transfers between devices  440 us (18%)
  matrix products  289 us (12%)
  local copies, waits for them, and re-layouts  114 us (5%)
  other arithmetic  52.2 us (2%)
  blocking collectives  35.4 us (1%)
    pallas_call x8, Pallas kernels, head_bwd(): pl.pallas_call(functools.partial(bwd_kernel, first=first, rows=rows, tok_...  791 us
    pallas_call x1, Pallas kernels, head_fwd(): pl.pallas_call(functools.partial(fwd_kernel, n_own=n_own, n_blk=n_blk, ro...  585 us
    all_gather x1, waiting for transfers between devices, local_step(): embed_full = lax.all_gather(emb_shard, 'fsdp', tiled=True)  219 us
    dot_general x3, matrix products, dot_last(): lax.dot_general(left_mat, right_mat, (((1,), (1,)), ((), ())), preferred_...  108 us
    dot_general x3, matrix products, dot_plain(): lax.dot_general(left_mat, right_mat, (((1,), (0,)), ((), ())), preferred_...  90.6 us
    dot_general x3, matrix products, dot_first(): lax.dot_general(left_mat, right_mat, (((0,), (0,)), ((), ())), preferred_...  90.6 us
    all_gather x1, waiting for transfers between devices, local_step(): d_x_all = lax.all_gather(d_x, 'fsdp', tiled=True)  75.5 us
    reduce_scatter x1, waiting for transfers between devices, local_step(): d_gate = lax.psum_scatter(d_gate, 'fsdp', scatter_dimension=0, tiled=True)  71.3 us
  transfers between devices with their start and end apart: 16, of which 5 were waited for; matrix products, arithmetic and copies ran while one was open for 17% of the time, Pallas kernels for 32%

profile of v1, /device:TPU:0, one launch (start us, length us, event | category | flops | bytes accessed | tf_op | source)
XLA Modules:
  0.0 2394.9 jit_solution(17315974866337083491)
XLA Ops:
  16.7 218.6 %all-gather.6.cloned.1.call-done = bf16[32128,768]{1,0:T(8,128)(2,1)} async-done(((bf16[4016,768]{1,0:T(8,128)(2,1)}), bf16[32128,768]{1,0:T(8,128)(2,1)}) %all-gather.6.cloned.1.call-update) | async-done | bytes 49348624 | tf_op jit(solution)/shard_map/all_gather | solution.py:318
  235.3 71.0 %gather_fusion = bf16[4096,768]{1,0:T(8,128)(2,1)} fusion(bf16[32128,768]{1,0:T(8,128)(2,1)} %all-gather.6.cloned.1.call-done, s32[4096]{0:T(1024)S(1)} %fusion.33), kind=kCustom, calls=%fused_computation | custom fusion | bytes 12599296 | tf_op jit(solution)/shard_map/jit(_take)/gather | solution.py:325
  312.3 27.8 %convolution_convert_fusion.1 = bf16[4096,3072]{1,0:T(8,128)(2,1)} fusion(bf16[768,3072]{1,0:T(8,128)(2,1)} %all-gather.8.cloned.1.call-done, f32[768]{0:T(1024)S(1)} %copy-done.24, f32[4096]{0:T(1024)S(1)} %get-tuple-element.68, bf16[4096,768]{1,0:T(8,128)(2,1)} %gather_fusion, pred[4096]{0:T(1024)(128)(4,1)S(1)} %compare_and_fusion.1), kind=kOutput, calls=%fused_computation.18 | convolution fusion | flops 19355664384 | bytes 36199424 | tf_op jit(solution)/shard_map/dot_general | solution.py:14
  340.1 37.0 %fusion = (bf16[4096,3072]{1,0:T(8,128)(2,1)}, bf16[4096,3072]{1,0:T(8,128)(2,1)}) fusion(bf16[4096,3072]{1,0:T(8,128)(2,1)} %convolution_convert_fusion.1, bf16[768,3072]{1,0:T(8,128)(2,1)} %all-gather.10.cloned.1.call-done, f32[768]{0:T(1024)S(1)} %copy-done.24, f32[4096]{0:T(1024)S(1)} %get-tuple-element.68, bf16[4096,768]{1,0:T(8,128)(2,1)} %gather_fusion, ...), kind=kOutput, calls=%fused_computation.7 | convolution fusion | flops 19456327680 | bytes 86531072 | tf_op jit(solution)/shard_map/dot_general | solution.py:14
  377.1 25.8 %fusion.24 = (f32[4096]{0:T(1024)S(1)}, bf16[4096,768]{1,0:T(8,128)(2,1)S(1)}) fusion(bf16[4096,3072]{1,0:T(8,128)(2,1)} %get-tuple-element.72, bf16[3072,768]{1,0:T(8,128)(2,1)} %all-gather.12.cloned.1.call-done, bf16[4096,768]{1,0:T(8,128)(2,1)} %gather_fusion, pred[4096]{0:T(1024)(128)(4,1)S(1)} %compare_and_fusion.1), kind=kOutput, calls=%fused_computation.40 | convolution fusion | flops 19358806016 | bytes 42487808 | tf_op jit(solution)/shard_map/dot_general | solution.py:14
  420.9 585.3 %shard_map.119 = (f32[1,4096]{1,0:T(1,128)}, bf16[8,768,4016]{2,1,0:T(8,128)(2,1)}) custom-call(bf16[8,4016,768]{2,1,0:T(8,128)(2,1)} %bitcast.57, bf16[768,4096]{1,0:T(8,128)(2,1)} %copy.47.hnt_ref.refs_1_), custom_call_target="tpu_custom_call" | custom-call | flops 202131898368 | bytes 98697216 | tf_op jit(solution)/shard_map/pallas_call | solution.py:138
  1006.2 98.2 %shard_map.120 = (f32[8,512,768]{2,1,0:T(8,128)}, f32[8,4096]{1,0:T(8,128)}, f32[768,4096]{1,0:T(8,128)}) custom-call(bf16[4096,768]{1,0:T(8,128)(2,1)} %fusion.23.refs_0_, bf16[768,4096]{1,0:T(8,128)(2,1)} %copy.47.hnt_ref.refs_1_, f32[1,4096]{1,0:T(1,128)} %get-tuple-element.37.refs_2_, s32[1,4096]{1,0:T(1,128)} %bitcast.70, ...), custom_call_target="tpu_custom_call" | custom-call | flops 77309411328 | bytes 52428800 | tf_op jit(solution)/shard_map/pallas_call | solution.py:239
  1104.5 98.9 %shard_map.121 = (f32[8,512,768]{2,1,0:T(8,128)}, f32[8,4096]{1,0:T(8,128)}, f32[768,4096]{1,0:T(8,128)}) custom-call(bf16[4096,768]{1,0:T(8,128)(2,1)} %fusion.23.refs_0_, bf16[768,4096]{1,0:T(8,128)(2,1)} %copy.47.hnt_ref.refs_1_, f32[1,4096]{1,0:T(1,128)} %get-tuple-element.37.refs_2_, s32[1,4096]{1,0:T(1,128)} %bitcast.71, ...), custom_call_target="tpu_custom_call", output_to_operand_aliasing={{2}: (6, {})} | custom-call | flops 77309411328 | bytes 52428800 | tf_op jit(solution)/shard_map/pallas_call | solution.py:239
  1203.5 98.9 %shard_map.122 = (f32[8,512,768]{2,1,0:T(8,128)}, f32[8,4096]{1,0:T(8,128)}, f32[768,4096]{1,0:T(8,128)}) custom-call(bf16[4096,768]{1,0:T(8,128)(2,1)} %fusion.23.refs_0_, bf16[768,4096]{1,0:T(8,128)(2,1)} %copy.47.hnt_ref.refs_1_, f32[1,4096]{1,0:T(1,128)} %get-tuple-element.37.refs_2_, s32[1,4096]{1,0:T(1,128)} %bitcast.72, ...), custom_call_target="tpu_custom_call", output_to_operand_aliasing={{2}: (6, {})} | custom-call | flops 77309411328 | bytes 52428800 | tf_op jit(solution)/shard_map/pallas_call | solution.py:239
  1302.5 99.1 %shard_map.123 = (f32[8,512,768]{2,1,0:T(8,128)}, f32[8,4096]{1,0:T(8,128)}, f32[768,4096]{1,0:T(8,128)}) custom-call(bf16[4096,768]{1,0:T(8,128)(2,1)} %fusion.23.refs_0_, bf16[768,4096]{1,0:T(8,128)(2,1)} %copy.47.hnt_ref.refs_1_, f32[1,4096]{1,0:T(1,128)} %get-tuple-element.37.refs_2_, s32[1,4096]{1,0:T(1,128)} %bitcast.73, ...), custom_call_target="tpu_custom_call", output_to_operand_aliasing={{2}: (6, {})} | custom-call | flops 77309411328 | bytes 52428800 | tf_op jit(solution)/shard_map/pallas_call | solution.py:239
  1401.7 98.9 %shard_map.124 = (f32[8,512,768]{2,1,0:T(8,128)}, f32[8,4096]{1,0:T(8,128)}, f32[768,4096]{1,0:T(8,128)}) custom-call(bf16[4096,768]{1,0:T(8,128)(2,1)} %fusion.23.refs_0_, bf16[768,4096]{1,0:T(8,128)(2,1)} %copy.47.hnt_ref.refs_1_, f32[1,4096]{1,0:T(1,128)} %get-tuple-element.37.refs_2_, s32[1,4096]{1,0:T(1,128)} %bitcast.74, ...), custom_call_target="tpu_custom_call", output_to_operand_aliasing={{2}: (6, {})} | custom-call | flops 77309411328 | bytes 52428800 | tf_op jit(solution)/shard_map/pallas_call | solution.py:239
  1500.7 98.9 %shard_map.125 = (f32[8,512,768]{2,1,0:T(8,128)}, f32[8,4096]{1,0:T(8,128)}, f32[768,4096]{1,0:T(8,128)}) custom-call(bf16[4096,768]{1,0:T(8,128)(2,1)} %fusion.23.refs_0_, bf16[768,4096]{1,0:T(8,128)(2,1)} %copy.47.hnt_ref.refs_1_, f32[1,4096]{1,0:T(1,128)} %get-tuple-element.37.refs_2_, s32[1,4096]{1,0:T(1,128)} %bitcast.75, ...), custom_call_target="tpu_custom_call", output_to_operand_aliasing={{2}: (6, {})} | custom-call | flops 77309411328 | bytes 52428800 | tf_op jit(solution)/shard_map/pallas_call | solution.py:239
  1599.7 99.0 %shard_map.126 = (f32[8,512,768]{2,1,0:T(8,128)}, f32[8,4096]{1,0:T(8,128)}, f32[768,4096]{1,0:T(8,128)}) custom-call(bf16[4096,768]{1,0:T(8,128)(2,1)} %fusion.23.refs_0_, bf16[768,4096]{1,0:T(8,128)(2,1)} %copy.47.hnt_ref.refs_1_, f32[1,4096]{1,0:T(1,128)} %get-tuple-element.37.refs_2_, s32[1,4096]{1,0:T(1,128)} %bitcast.76, ...), custom_call_target="tpu_custom_call", output_to_operand_aliasing={{2}: (6, {})} | custom-call | flops 77309411328 | bytes 52428800 | tf_op jit(solution)/shard_map/pallas_call | solution.py:239
  1698.7 99.0 %shard_map.127 = (f32[8,432,768]{2,1,0:T(8,128)}, f32[8,4096]{1,0:T(8,128)}, f32[768,4096]{1,0:T(8,128)}) custom-call(bf16[4096,768]{1,0:T(8,128)(2,1)} %fusion.23.refs_0_, bf16[768,4096]{1,0:T(8,128)(2,1)} %copy.47.hnt_ref.refs_1_, f32[1,4096]{1,0:T(1,128)} %get-tuple-element.37.refs_2_, s32[1,4096]{1,0:T(1,128)} %bitcast.77, ...), custom_call_target="tpu_custom_call", output_to_operand_aliasing={{2}: (6, {})} | custom-call | flops 65229815808 | bytes 52428800 | tf_op jit(solution)/shard_map/pallas_call | solution.py:239
  1818.6 49.6 %fusion.9 = (bf16[4096,3072]{1,0:T(8,128)(2,1)}, bf16[4096,3072]{1,0:T(8,128)(2,1)}) fusion(bf16[4096,3072]{1,0:T(8,128)(2,1)} %convolution_convert_fusion.1, bf16[4096,3072]{1,0:T(8,128)(2,1)} %get-tuple-element.73, bf16[3072,768]{1,0:T(8,128)(2,1)} %all-gather.12.cloned.1.call-done, f32[4096]{0:T(1024)S(1)} %broadcast_multiply_fusion.2, ...), kind=kOutput, calls=%fused_computation.16 | convolution fusion | flops 19538116608 | bytes 124308480 | tf_op jit(solution)/shard_map/dot_general | solution.py:18
  1868.3 26.1 %fusion.42 = f32[4096,768]{1,0:T(8,128)} fusion(bf16[4096,3072]{1,0:T(8,128)(2,1)} %get-tuple-element.66, bf16[768,3072]{1,0:T(8,128)(2,1)} %all-gather.8.cloned.1.call-done), kind=kOutput, calls=%fused_computation.78 | convolution fusion | flops 19327352832 | bytes 42467328 | tf_op jit(solution)/shard_map/dot_general | solution.py:18
  1894.4 32.5 %fusion.15 = (f32[4096]{0:T(1024)S(1)}, f32[4096,768]{1,0:T(8,128)}) fusion(bf16[4096,768]{1,0:T(8,128)(2,1)} %gather_fusion, pred[4096]{0:T(1024)(128)(4,1)S(1)} %copy-done.20, f32[768]{0:T(1024)S(1)} %copy-done.25, f32[4096,768]{1,0:T(8,128)} %fusion.42, bf16[4096,3072]{1,0:T(8,128)(2,1)} %get-tuple-element.65, ...), kind=kOutput, calls=%fused_computation.31 | convolution fusion | flops 19349368832 | bytes 61365248 | tf_op jit(solution)/shard_map/dot_general | solution.py:18
  1944.2 30.6 %fusion.28 = f32[3072,768]{1,0:T(8,128)} fusion(bf16[4096,3072]{1,0:T(8,128)(2,1)} %get-tuple-element.72, bf16[4096,768]{1,0:T(8,128)(2,1)} %copy-done, f32[768,4096]{0,1:T(8,128)} %copy.56, f32[4096]{0:T(1024)S(1)} %copy-done.3, f32[4096]{0:T(1024)S(1)} %broadcast_multiply_fusion.2, f32[4096]{0:T(1024)S(1)} %copy-done.14, f32[768]{0:T(1024)S(1)} %copy-done.18), kind=kOutput, calls=%fused_computation.48 | convolution fusion | flops 19349372928 | bytes 53529600 | tf_op jit(solution)/shard_map/dot_general | solution.py:22
  1974.8 29.8 %fusion.34 = f32[768,3072]{1,0:T(8,128)} fusion(bf16[4096,3072]{1,0:T(8,128)(2,1)} %get-tuple-element.65, f32[768]{0:T(1024)S(1)} %copy-done.25, f32[4096]{0:T(1024)S(1)} %copy-done.23, bf16[4096,768]{1,0:T(8,128)(2,1)} %gather_fusion, pred[4096]{0:T(1024)(128)(4,1)S(1)} %copy-done.20), kind=kOutput, calls=%fused_computation.76 | convolution fusion | flops 19343081472 | bytes 40918016 | tf_op jit(solution)/shard_map/dot_general | solution.py:22
  2004.8 30.2 %fusion.36 = f32[768,3072]{1,0:T(8,128)} fusion(bf16[4096,3072]{1,0:T(8,128)(2,1)} %get-tuple-element.66, f32[768]{0:T(1024)S(1)} %copy-done.25, f32[4096]{0:T(1024)S(1)} %copy-done.23, bf16[4096,768]{1,0:T(8,128)(2,1)} %gather_fusion, pred[4096]{0:T(1024)(128)(4,1)S(1)} %copy-done.20), kind=kOutput, calls=%fused_computation.77 | convolution fusion | flops 19343081472 | bytes 40918016 | tf_op jit(solution)/shard_map/dot_general | solution.py:22
  2097.7 75.5 %all-gather.14.cloned.1.call-done.dx_hbm = bf16[32768,768]{1,0:T(8,128)(2,1)} async-done(((bf16[4096,768]{1,0:T(8,128)(2,1)}), bf16[32768,768]{1,0:T(8,128)(2,1)}) %all-gather.14.cloned.1.call-update) | async-done | bytes 50331664 | tf_op jit(solution)/shard_map/all_gather | solution.py:343
  2173.1 70.5 %shard_map.128 = f32[4016,768]{1,0:T(8,128)} custom-call(s32[2]{0:T(128)} %pad_add_fusion.meta_ref, s32[128]{0:T(128)} %get-tuple-element.55.live_ref, s32[1,32768]{1,0:T(1,128)} %bitcast.66, bf16[32768,768]{1,0:T(8,128)(2,1)} %all-gather.14.cloned.1.call-done.dx_hbm, f32[4016,768]{1,0:T(8,128)} %bitcast_dynamic-update-slice_fusion.7.base_ref), custom_call_target="tpu_custom_call" | custom-call | flops 50532974592 | bytes 24674304 | tf_op jit(solution)/shard_map/pallas_call | solution.py:294
  2244.4 71.3 %reduce-scatter.30.cloned.1.call-done = f32[96,3072]{1,0:T(8,128)} async-done(((f32[768,3072]{1,0:T(8,128)}), f32[96,3072]{1,0:T(8,128)}) %reduce-scatter.30.cloned.1.call-update) | async-done | bytes 1179664 | tf_op jit(solution)/shard_map/reduce_scatter | solution.py:341
  2315.7 71.3 %reduce-scatter.28.cloned.1.call-done = f32[96,3072]{1,0:T(8,128)} async-done(((f32[768,3072]{1,0:T(8,128)}), f32[96,3072]{1,0:T(8,128)}) %reduce-scatter.28.cloned.1.call-update) | async-done | bytes 1179664 | tf_op jit(solution)/shard_map/reduce_scatter | solution.py:340
  (131 shorter events, 134.6 us)
Async XLA Ops:
  7.2 228.2 %all-gather.6.cloned.1.call-start = ((), (), s32[]{:S(2)}) async-start(), calls=%async_computation.11 | async-start | bytes 55517184 | tf_op jit(solution)/shard_map/all_gather | solution.py:318
  7.9 304.4 %all-gather.8.cloned.1.call-start = ((), (), s32[]{:S(2)}) async-start(), calls=%async_computation.12 | async-start | bytes 5308416 | tf_op jit(solution)/shard_map/all_gather | solution.py:319
  8.6 331.5 %all-gather.10.cloned.1.call-start = ((), (), s32[]{:S(2)}) async-start(), calls=%async_computation.13 | async-start | bytes 5308416 | tf_op jit(solution)/shard_map/all_gather | solution.py:320
  9.4 367.7 %all-gather.12.cloned.1.call-start = ((), (), s32[]{:S(2)}) async-start(), calls=%async_computation.14 | async-start | bytes 5308416 | tf_op jit(solution)/shard_map/all_gather | solution.py:321
  10.0 2066.5 %reduce-scatter.12.cloned.1.call-start = ((), (), s32[]{:S(2)}) async-start(), calls=%async_computation.16 | async-start | bytes 14155776 | tf_op jit(solution)/shard_map/reduce_scatter | solution.py:335
  16.7 289.7 %copy-start.4 = (s32[4096]{0:T(1024)}, s32[4096]{0:T(1024)S(1)}, u32[]{:S(2)}) copy-start(s32[4096]{0:T(1024)S(1)} %get-tuple-element.36) | copy-start | bytes 49156
  16.7 360.4 %copy-start.19 = (pred[4096]{0:T(1024)(128)(4,1)}, pred[4096]{0:T(1024)(128)(4,1)S(1)}, u32[]{:S(2)}) copy-start(pred[4096]{0:T(1024)(128)(4,1)S(1)} %compare_and_fusion.1) | copy-start | bytes 12292
  16.7 295.6 %copy-start.24 = (f32[768]{0:T(1024)S(1)}, f32[768]{0:T(1024)}, u32[]{:S(2)}) copy-start(f32[768]{0:T(1024)} %param.14) | copy-start | bytes 9220
  1104.4 974.7 %reduce-scatter.14.cloned.1.call-start = ((), (), s32[]{:S(2)}) async-start(), calls=%async_computation.17 | async-start | bytes 14155776 | tf_op jit(solution)/shard_map/reduce_scatter | solution.py:335
  1203.4 878.4 %reduce-scatter.16.cloned.1.call-start = ((), (), s32[]{:S(2)}) async-start(), calls=%async_computation.18 | async-start | bytes 14155776 | tf_op jit(solution)/shard_map/reduce_scatter | solution.py:335
  1302.5 782.0 %reduce-scatter.18.cloned.1.call-start = ((), (), s32[]{:S(2)}) async-start(), calls=%async_computation.19 | async-start | bytes 14155776 | tf_op jit(solution)/shard_map/reduce_scatter | solution.py:335
  1401.7 685.5 %reduce-scatter.20.cloned.1.call-start = ((), (), s32[]{:S(2)}) async-start(), calls=%async_computation.20 | async-start | bytes 14155776 | tf_op jit(solution)/shard_map/reduce_scatter | solution.py:335
  1500.7 589.1 %reduce-scatter.22.cloned.1.call-start = ((), (), s32[]{:S(2)}) async-start(), calls=%async_computation.21 | async-start | bytes 14155776 | tf_op jit(solution)/shard_map/reduce_scatter | solution.py:335
  1599.6 492.8 %reduce-scatter.24.cloned.1.call-start = ((), (), s32[]{:S(2)}) async-start(), calls=%async_computation.22 | async-start | bytes 14155776 | tf_op jit(solution)/shard_map/reduce_scatter | solution.py:335
  1698.7 396.5 %reduce-scatter.26.cloned.1.call-start = ((), (), s32[]{:S(2)}) async-start(), calls=%async_computation.23 | async-start | bytes 11943936 | tf_op jit(solution)/shard_map/reduce_scatter | solution.py:335
  1818.6 354.6 %all-gather.14.cloned.1.call-start = ((), (), s32[]{:S(2)}) async-start(), calls=%async_computation.15 | async-start | bytes 56623104 | tf_op jit(solution)/shard_map/all_gather | solution.py:343
  1944.1 300.3 %reduce-scatter.32.cloned.1.call-start = ((), (), s32[]{:S(2)}) async-start(), calls=%async_computation.26 | async-start | bytes 10616832 | tf_op jit(solution)/shard_map/reduce_scatter | solution.py:342
  1974.7 341.0 %reduce-scatter.30.cloned.1.call-start = ((), (), s32[]{:S(2)}) async-start(), calls=%async_computation.25 | async-start | bytes 10616832 | tf_op jit(solution)/shard_map/reduce_scatter | solution.py:341
  2004.7 44.6 %copy-start.6 = (f32[8,4096]{1,0:T(8,128)S(1)}, f32[8,4096]{1,0:T(8,128)}, u32[]{:S(2)}) copy-start(f32[8,4096]{1,0:T(8,128)} %get-tuple-element.40) | copy-start | bytes 393220
  2004.7 44.5 %copy-start.7 = (f32[8,4096]{1,0:T(8,128)S(1)}, f32[8,4096]{1,0:T(8,128)}, u32[]{:S(2)}) copy-start(f32[8,4096]{1,0:T(8,128)} %get-tuple-element.42) | copy-start | bytes 393220
  2004.7 44.5 %copy-start.8 = (f32[8,4096]{1,0:T(8,128)S(1)}, f32[8,4096]{1,0:T(8,128)}, u32[]{:S(2)}) copy-start(f32[8,4096]{1,0:T(8,128)} %get-tuple-element.44) | copy-start | bytes 393220
  2004.7 44.6 %copy-start.21 = (f32[1,4096]{1,0:T(1,128)S(1)}, f32[1,4096]{1,0:T(1,128)}, u32[]{:S(2)}) copy-start(f32[1,4096]{1,0:T(1,128)} %get-tuple-element.37.refs_2_) | copy-start | bytes 49156
  2004.7 382.3 %reduce-scatter.28.cloned.1.call-start = ((), (), s32[]{:S(2)}) async-start(), calls=%async_computation.24 | async-start | bytes 10616832 | tf_op jit(solution)/shard_map/reduce_scatter | solution.py:340
  2047.1 50.5 %copy-start.1 = (s32[32768]{0:T(1024)}, s32[32768]{0:T(1024)S(1)}, u32[]{:S(2)}) copy-start(s32[32768]{0:T(1024)S(1)} %all_gather.22) | copy-start | bytes 393220
  (18 other events, 494.0 us)
Sparse Core Ops, SparseCore 0:
  9.8 225.4 all-gather.5
  237.2 32.9 all-gather.7
  271.9 32.9 all-gather.9
  306.6 32.9 all-gather.11
  1104.6 82.5 reduce-scatter.11
  1203.6 82.5 reduce-scatter.13
  1302.6 82.5 reduce-scatter.15
  1401.8 82.5 reduce-scatter.17
  1500.8 82.5 reduce-scatter.19
  1599.8 82.4 reduce-scatter.21
  1698.8 82.5 reduce-scatter.23
  1818.7 73.0 reduce-scatter.25
  1944.2 228.8 all-gather.13
  2177.0 67.4 reduce-scatter.31
  2248.3 67.4 reduce-scatter.29
  2319.6 67.4 reduce-scatter.27

commit v2 on v1

--- a/solution.py
+++ b/solution.py
@@ -285,7 +285,7 @@
     out_ref[...] = base_ref[...] + out_ref[...] * scale
 
 
-def scatter_rows(ids, d_x, base, first_row, scale, rows=1024, toks=256):
+def scatter_rows(ids, d_x, base, first_row, scale, rows=1024, toks=640):
     per, dim = base.shape
     n_blk = ids.shape[0] // toks
     live = jnp.any(((ids >= first_row) & (ids < first_row + per)).reshape(n_blk, toks), axis=1)
@@ -305,6 +305,12 @@
     )(meta, order, ids.reshape(1, -1), d_x, base)
 
 
+def exchange_plan(ids_all, group, per):
+    owners = jnp.arange(group, dtype=jnp.int32)
+    counts = jnp.sum((ids_all[:, None, :] // per == owners[None, :, None]).astype(jnp.int32), axis=2)
+    return counts, jnp.cumsum(counts, axis=1) - counts
+
+
 def solution(mesh):
     group = mesh.shape['fsdp']
 
@@ -320,15 +326,19 @@
         w_up = lax.all_gather(up_shard, 'fsdp', tiled=True)
         w_down = lax.all_gather(down_shard, 'fsdp', tiled=True)
 
-        ids_all = lax.all_gather(ids_flat, 'fsdp', tiled=True)
+        ids_all = lax.all_gather(ids_flat, 'fsdp')
+        counts, starts = exchange_plan(ids_all, group, per)
+        cap = -(-n_tok * 5 // (group * 4 * 128)) * 128
+        rounds = (jnp.max(counts) + cap - 1) // cap
+        pad_ids = jnp.pad(ids_all, ((0, 0), (0, cap)), constant_values=-1)
 
         x_emb = jnp.take(embed_full, ids_flat, axis=0, indices_are_sorted=True).astype(jnp.float32) * emb_scale
         hid_norm, saved = mlp_forward(x_emb, w_gate, w_up, w_down, gain_mlp, gain_final)
         hid_t = hid_norm.T
         emb3 = embed_full.reshape(group, per, model_dim)
-        log_norm, emb_t = head_fwd(emb3, hid_t)
+        log_norm, emb_t = head_fwd(emb3, hid_t, rows=1024)
         labels = lab_flat.reshape(1, -1)
-        block = 512
+        block = 768
         d_hid_t, lab_logit, d_rows = None, 0.0, []
         for chunk in range(pl.cdiv(per, block)):
             d_emb, lab_part, d_hid_t = head_bwd(hid_norm, hid_t, log_norm, labels, emb3, emb_t, d_hid_t, chunk, block=block, tok_tile=1024, sub=1, inv_count=inv_count)
@@ -340,8 +350,16 @@
         d_gate = lax.psum_scatter(d_gate, 'fsdp', scatter_dimension=0, tiled=True)
         d_up = lax.psum_scatter(d_up, 'fsdp', scatter_dimension=0, tiled=True)
         d_down = lax.psum_scatter(d_down, 'fsdp', scatter_dimension=0, tiled=True)
-        d_x_all = lax.all_gather(d_x, 'fsdp', tiled=True)
-        d_embed = scatter_rows(ids_all, d_x_all, jnp.concatenate(d_rows, axis=0), me * per, emb_scale)
+        pad_d_x = jnp.pad(d_x, ((0, cap), (0, 0)))
+
+        def exchange_round(turn, d_embed):
+            send = jnp.concatenate([lax.dynamic_slice(pad_d_x, (starts[me, own] + turn * cap, 0), (cap, model_dim)) for own in range(group)], axis=0)
+            ids = jnp.concatenate([lax.dynamic_slice(pad_ids, (src, starts[src, me] + turn * cap), (1, cap)) for src in range(group)], axis=1)
+            got = lax.all_to_all(send, 'fsdp', 0, 0, tiled=True)
+            return scatter_rows(ids.reshape(-1), got, d_embed, me * per, emb_scale, toks=cap)
+
+        d_embed = exchange_round(0, jnp.concatenate(d_rows, axis=0))
+        d_embed = lax.fori_loop(1, rounds, exchange_round, d_embed)
         return loss, d_embed, d_gate, d_up, d_down
 
     shard_spec = P('fsdp', None)

time: 2410 us -> 2230 us (0.925)
  waiting for transfers between devices: 440 us -> 221 us
  Pallas kernels: 1450 us -> 1340 us
  blocking collectives: 35.4 us -> 132 us
  local copies, waits for them, and re-layouts: 114 us -> 147 us
  between operations: 16.4 us -> 47.1 us
    psum x1, blocking collectives: 23.3 us -> 120 us  [local_step(): lax.psum(jnp.sum(log_norm[0] - jnp.sum(lab_logit, axis=0)), 'fsdp')]
    all_gather x1 -> x0, waiting for transfers between devices: 75.5 us -> none  [local_step(): d_x_all = lax.all_gather(d_x, 'fsdp', tiled=True)]
    reduce_scatter x1, waiting for transfers between devices: 71.3 us -> 0.02 us  [local_step(): d_gate = lax.psum_scatter(d_gate, 'fsdp', scatter_dimension=0, tiled=True)]
    reduce_scatter x1, waiting for transfers between devices: 71.3 us -> 0.02 us  [local_step(): d_up = lax.psum_scatter(d_up, 'fsdp', scatter_dimension=0, tiled=True)]
    pallas_call x1, Pallas kernels: 585 us -> 535 us  [head_fwd(): pl.pallas_call(functools.partial(fwd_kernel, n_own=n_own, n_blk=n_blk, ro...]
    pallas_call x8 -> x6, Pallas kernels: 791 us -> 744 us  [head_bwd(): pl.pallas_call(functools.partial(bwd_kernel, first=first, rows=rows, tok_...]
    gather x1 -> x2, local copies, waits for them, and re-layouts: 71 us -> 79.6 us  [local_step(): jnp.take(embed_full, ids_flat, axis=0, indices_are_sorted=True)]
  transfers between devices with their start and end apart: 16 -> 14, of which waited for: 5 -> 1; matrix products, arithmetic and copies ran while one was open for 17% -> 20% of each run, Pallas kernels for 32% -> 30%
where the time goes in v2:
time: 2230 us
  Pallas kernels  1340 us (60%)
  matrix products  284 us (13%)
  waiting for transfers between devices  221 us (10%)
  local copies, waits for them, and re-layouts  147 us (7%)
  blocking collectives  132 us (6%)
  other arithmetic  52.3 us (2%)
  between operations  47.1 us (2%)
    pallas_call x6, Pallas kernels, head_bwd(): pl.pallas_call(functools.partial(bwd_kernel, first=first, rows=rows, tok_...  744 us
    pallas_call x1, Pallas kernels, head_fwd(): pl.pallas_call(functools.partial(fwd_kernel, n_own=n_own, n_blk=n_blk, ro...  535 us
    all_gather x1, waiting for transfers between devices, local_step(): embed_full = lax.all_gather(emb_shard, 'fsdp', tiled=True)  219 us
    psum x1, blocking collectives, local_step(): lax.psum(jnp.sum(log_norm[0] - jnp.sum(lab_logit, axis=0)), 'fsdp')  120 us
    dot_general x3, matrix products, dot_last(): lax.dot_general(left_mat, right_mat, (((1,), (1,)), ((), ())), preferred_...  105 us
    dot_general x3, matrix products, dot_plain(): lax.dot_general(left_mat, right_mat, (((1,), (0,)), ((), ())), preferred_...  96.1 us
    dot_general x3, matrix products, dot_first(): lax.dot_general(left_mat, right_mat, (((0,), (0,)), ((), ())), preferred_...  83.1 us
    gather x2, local copies, waits for them, and re-layouts, local_step(): jnp.take(embed_full, ids_flat, axis=0, indices_are_sorted=True)  79.6 us
  transfers between devices with their start and end apart: 14, of which 1 were waited for; matrix products, arithmetic and copies ran while one was open for 20% of the time, Pallas kernels for 30%

profile of v2, /device:TPU:0, one launch (start us, length us, event | category | flops | bytes accessed | tf_op | source)
XLA Modules:
  0.0 2228.8 jit_solution(3448345555795992426)
XLA Ops:
  16.7 218.6 %all-gather.6.cloned.1.call-done = bf16[32128,768]{1,0:T(8,128)(2,1)} async-done(((bf16[4016,768]{1,0:T(8,128)(2,1)}), bf16[32128,768]{1,0:T(8,128)(2,1)}) %all-gather.6.cloned.1.call-update) | async-done | bytes 49348624 | tf_op jit(solution)/shard_map/all_gather | solution.py:324
  235.3 71.1 %gather_fusion = bf16[4096,768]{1,0:T(8,128)(2,1)} fusion(bf16[32128,768]{1,0:T(8,128)(2,1)} %all-gather.6.cloned.1.call-done, s32[4096]{0:T(1024)S(1)} %fusion.34), kind=kCustom, calls=%fused_computation | custom fusion | bytes 12599296 | tf_op jit(solution)/shard_map/jit(_take)/gather | solution.py:335
  320.5 28.4 %convolution_convert_fusion.1 = bf16[4096,3072]{1,0:T(8,128)(2,1)} fusion(bf16[768,3072]{1,0:T(8,128)(2,1)} %all-gather.8.cloned.1.call-done, f32[768]{0:T(1024)S(1)} %copy-done.35, f32[4096]{0:T(1024)S(1)} %get-tuple-element.343, bf16[4096,768]{0,1:T(8,128)(2,1)} %copy.40, pred[4096]{0:T(1024)(128)(4,1)S(1)} %compare_and_fusion), kind=kOutput, calls=%fused_computation.37 | convolution fusion | flops 19355664384 | bytes 36199424 | tf_op jit(solution)/shard_map/dot_general | solution.py:14
  348.9 40.4 %fusion = (bf16[4096,3072]{1,0:T(8,128)(2,1)}, bf16[4096,3072]{1,0:T(8,128)(2,1)}) fusion(bf16[4096,3072]{1,0:T(8,128)(2,1)} %convolution_convert_fusion.1, bf16[768,3072]{1,0:T(8,128)(2,1)} %all-gather.10.cloned.1.call-done, f32[768]{0:T(1024)S(1)} %copy-done.35, f32[4096]{0:T(1024)S(1)} %get-tuple-element.343, bf16[4096,768]{0,1:T(8,128)(2,1)} %copy.40, ...), kind=kOutput, calls=%fused_computation.26 | convolution fusion | flops 19456327680 | bytes 86531072 | tf_op jit(solution)/shard_map/dot_general | solution.py:14
  389.3 27.3 %fusion.24 = (f32[4096]{0:T(1024)S(1)}, bf16[4096,768]{0,1:T(8,128)(2,1)S(1)}) fusion(bf16[4096,3072]{1,0:T(8,128)(2,1)} %get-tuple-element.365, bf16[3072,768]{1,0:T(8,128)(2,1)} %all-gather.12.cloned.1.call-done, bf16[4096,768]{0,1:T(8,128)(2,1)} %copy.40, pred[4096]{0:T(1024)(128)(4,1)S(1)} %compare_and_fusion), kind=kOutput, calls=%fused_computation.59 | convolution fusion | flops 19358806016 | bytes 42487808 | tf_op jit(solution)/shard_map/dot_general | solution.py:14
  436.8 534.8 %shard_map.119 = (f32[1,4096]{1,0:T(1,128)}, bf16[8,768,4016]{2,1,0:T(8,128)(2,1)}) custom-call(bf16[8,4016,768]{2,1,0:T(8,128)(2,1)} %bitcast.131, bf16[768,4096]{1,0:T(8,128)(2,1)} %fusion.57.hnt_ref.refs_1_), custom_call_target="tpu_custom_call" | custom-call | flops 202131898368 | bytes 98697216 | tf_op jit(solution)/shard_map/pallas_call | solution.py:138
  971.7 137.9 %shard_map.120 = (f32[8,768,768]{2,1,0:T(8,128)}, f32[8,4096]{1,0:T(8,128)}, f32[768,4096]{1,0:T(8,128)}) custom-call(bf16[4096,768]{1,0:T(8,128)(2,1)} %copy.41.refs_0_, bf16[768,4096]{1,0:T(8,128)(2,1)} %fusion.57.hnt_ref.refs_1_, f32[1,4096]{1,0:T(1,128)} %get-tuple-element.202.refs_2_, s32[1,4096]{1,0:T(1,128)} %bitcast.142, ...), custom_call_target="tpu_custom_call" | custom-call | flops 115964116992 | bytes 52428800 | tf_op jit(solution)/shard_map/pallas_call | solution.py:239
  1109.6 138.6 %shard_map.121 = (f32[8,768,768]{2,1,0:T(8,128)}, f32[8,4096]{1,0:T(8,128)}, f32[768,4096]{1,0:T(8,128)}) custom-call(bf16[4096,768]{1,0:T(8,128)(2,1)} %copy.41.refs_0_, bf16[768,4096]{1,0:T(8,128)(2,1)} %fusion.57.hnt_ref.refs_1_, f32[1,4096]{1,0:T(1,128)} %get-tuple-element.202.refs_2_, s32[1,4096]{1,0:T(1,128)} %bitcast.143, ...), custom_call_target="tpu_custom_call", output_to_operand_aliasing={{2}: (6, {})} | custom-call | flops 115964116992 | bytes 52428800 | tf_op jit(solution)/shard_map/pallas_call | solution.py:239
  1248.3 139.0 %shard_map.122 = (f32[8,768,768]{2,1,0:T(8,128)}, f32[8,4096]{1,0:T(8,128)}, f32[768,4096]{1,0:T(8,128)}) custom-call(bf16[4096,768]{1,0:T(8,128)(2,1)} %copy.41.refs_0_, bf16[768,4096]{1,0:T(8,128)(2,1)} %fusion.57.hnt_ref.refs_1_, f32[1,4096]{1,0:T(1,128)} %get-tuple-element.202.refs_2_, s32[1,4096]{1,0:T(1,128)} %bitcast.144, ...), custom_call_target="tpu_custom_call", output_to_operand_aliasing={{2}: (6, {})} | custom-call | flops 115964116992 | bytes 52428800 | tf_op jit(solution)/shard_map/pallas_call | solution.py:239
  1387.4 138.7 %shard_map.123 = (f32[8,768,768]{2,1,0:T(8,128)}, f32[8,4096]{1,0:T(8,128)}, f32[768,4096]{1,0:T(8,128)}) custom-call(bf16[4096,768]{1,0:T(8,128)(2,1)} %copy.41.refs_0_, bf16[768,4096]{1,0:T(8,128)(2,1)} %fusion.57.hnt_ref.refs_1_, f32[1,4096]{1,0:T(1,128)} %get-tuple-element.202.refs_2_, s32[1,4096]{1,0:T(1,128)} %bitcast.145, ...), custom_call_target="tpu_custom_call", output_to_operand_aliasing={{2}: (6, {})} | custom-call | flops 115964116992 | bytes 52428800 | tf_op jit(solution)/shard_map/pallas_call | solution.py:239
  1526.2 138.6 %shard_map.124 = (f32[8,768,768]{2,1,0:T(8,128)}, f32[8,4096]{1,0:T(8,128)}, f32[768,4096]{1,0:T(8,128)}) custom-call(bf16[4096,768]{1,0:T(8,128)(2,1)} %copy.41.refs_0_, bf16[768,4096]{1,0:T(8,128)(2,1)} %fusion.57.hnt_ref.refs_1_, f32[1,4096]{1,0:T(1,128)} %get-tuple-element.202.refs_2_, s32[1,4096]{1,0:T(1,128)} %bitcast.146, ...), custom_call_target="tpu_custom_call", output_to_operand_aliasing={{2}: (6, {})} | custom-call | flops 115964116992 | bytes 52428800 | tf_op jit(solution)/shard_map/pallas_call | solution.py:239
  1665.5 11.1 all-gather
  1678.4 51.5 %shard_map.125 = (f32[8,176,768]{2,1,0:T(8,128)}, f32[8,4096]{1,0:T(8,128)}, f32[768,4096]{1,0:T(8,128)}) custom-call(bf16[4096,768]{1,0:T(8,128)(2,1)} %copy.41.refs_0_, bf16[768,4096]{1,0:T(8,128)(2,1)} %fusion.57.hnt_ref.refs_1_, f32[1,4096]{1,0:T(1,128)} %get-tuple-element.202.refs_2_, s32[1,4096]{1,0:T(1,128)} %bitcast.147, ...), custom_call_target="tpu_custom_call", output_to_operand_aliasing={{2}: (6, {})} | custom-call | flops 26575110144 | bytes 52428800 | tf_op jit(solution)/shard_map/pallas_call | solution.py:239
  1729.9 9.1 fusion.25
  1739.1 30.2 %fusion.28 = f32[3072,768]{1,0:T(8,128)} fusion(bf16[4096,3072]{1,0:T(8,128)(2,1)} %get-tuple-element.365, bf16[4096,768]{0,1:T(8,128)(2,1)} %copy-done.2, f32[768,4096]{1,0:T(8,128)} %get-tuple-element.217, f32[4096]{0:T(1024)S(1)} %copy-done.7, f32[4096]{0:T(1024)S(1)} %broadcast_multiply_fusion.2, f32[4096]{0:T(1024)S(1)} %copy-done.17, ...), kind=kOutput, calls=%fused_computation.67 | convolution fusion | flops 19349372928 | bytes 53529600 | tf_op jit(solution)/shard_map/dot_general | solution.py:22
  1769.9 50.7 %fusion.9 = (bf16[4096,3072]{1,0:T(8,128)(2,1)}, bf16[4096,3072]{1,0:T(8,128)(2,1)}) fusion(bf16[4096,3072]{1,0:T(8,128)(2,1)} %convolution_convert_fusion.1, bf16[4096,3072]{1,0:T(8,128)(2,1)} %get-tuple-element.366, bf16[3072,768]{1,0:T(8,128)(2,1)} %all-gather.12.cloned.1.call-done, f32[4096]{0:T(1024)S(1)} %broadcast_multiply_fusion.2, ...), kind=kOutput, calls=%fused_computation.35 | convolution fusion | flops 19538116608 | bytes 124308480 | tf_op jit(solution)/shard_map/dot_general | solution.py:18
  1820.6 27.3 %fusion.37 = f32[768,3072]{1,0:T(8,128)} fusion(bf16[4096,3072]{1,0:T(8,128)(2,1)} %get-tuple-element.340, f32[768]{0:T(1024)S(1)} %copy-done.36, f32[4096]{0:T(1024)S(1)} %copy-done.34, bf16[4096,768]{0,1:T(8,128)(2,1)} %copy.40, pred[4096]{0:T(1024)(128)(4,1)S(1)} %copy-done.30), kind=kOutput, calls=%fused_computation.139 | convolution fusion | flops 19343081472 | bytes 40918016 | tf_op jit(solution)/shard_map/dot_general | solution.py:22
  1864.4 26.2 %fusion.44 = f32[4096,768]{0,1:T(8,128)} fusion(bf16[4096,3072]{1,0:T(8,128)(2,1)} %get-tuple-element.341, bf16[768,3072]{1,0:T(8,128)(2,1)} %all-gather.8.cloned.1.call-done), kind=kOutput, calls=%fused_computation.142 | convolution fusion | flops 19327352832 | bytes 42467328 | tf_op jit(solution)/shard_map/dot_general | solution.py:18
  1890.6 28.0 %fusion.15 = (f32[4096]{0:T(1024)S(1)}, f32[4096,768]{0,1:T(8,128)}) fusion(bf16[4096,768]{0,1:T(8,128)(2,1)S(1)} %bitcast.139, pred[4096]{0:T(1024)(128)(4,1)S(1)} %copy-done.30, f32[768]{0:T(1024)S(1)} %copy-done.36, f32[4096,768]{0,1:T(8,128)} %fusion.44, bf16[4096,3072]{1,0:T(8,128)(2,1)} %get-tuple-element.340, ...), kind=kOutput, calls=%fused_computation.50 | convolution fusion | flops 19349368832 | bytes 61365248 | tf_op jit(solution)/shard_map/dot_general | solution.py:18
  1918.7 25.6 %fusion.39 = f32[768,3072]{1,0:T(8,128)} fusion(bf16[4096,3072]{1,0:T(8,128)(2,1)} %get-tuple-element.341, f32[768]{0:T(1024)S(1)} %copy-done.36, f32[4096]{0:T(1024)S(1)} %copy-done.34, bf16[4096,768]{0,1:T(8,128)(2,1)S(1)} %bitcast.139, pred[4096]{0:T(1024)(128)(4,1)S(1)} %copy-done.30), kind=kOutput, calls=%fused_computation.140 | convolution fusion | flops 19343081472 | bytes 40918016 | tf_op jit(solution)/shard_map/dot_general | solution.py:22
  1944.4 14.0 fusion.21
  1970.6 10.7 copy.53
  2006.3 120.5 %psum.7 = f32[]{:T(128)} all-reduce(f32[]{:T(128)} %subtract_reduce_fusion), channel_id=1, replica_groups=mesh['fsdp'=8] {'fsdp'}, use_global_device_ids=true, to_apply=%region_5.6 | all-reduce | flops 1 | bytes 8 | tf_op jit(solution)/shard_map/psum | solution.py:347
  2160.3 60.5 %shard_map.126 = f32[4016,768]{1,0:T(8,128)} custom-call(s32[2]{0:T(128)} %pad_add_fusion.1.meta_ref, s32[8]{0:T(128)} %get-tuple-element.216.live_ref, s32[1,5120]{1,0:T(1,128)} %copy-done.31, bf16[5120,768]{1,0:T(8,128)(2,1)} %bitcast.46.dx_hbm, f32[4016,768]{1,0:T(8,128)} %bitcast_dynamic-update-slice_fusion.5.base_ref), custom_call_target="tpu_custom_call" | custom-call | flops 50532974592 | bytes 24674304 | tf_op jit(solution)/shard_map/pallas_call | solution.py:294
  (170 shorter events, 102.9 us)
Async XLA Ops:
  7.2 228.2 %all-gather.6.cloned.1.call-start = ((), (), s32[]{:S(2)}) async-start(), calls=%async_computation.11 | async-start | bytes 55517184 | tf_op jit(solution)/shard_map/all_gather | solution.py:324
  7.9 312.6 %all-gather.8.cloned.1.call-start = ((), (), s32[]{:S(2)}) async-start(), calls=%async_computation.12 | async-start | bytes 5308416 | tf_op jit(solution)/shard_map/all_gather | solution.py:325
  8.6 340.2 %all-gather.10.cloned.1.call-start = ((), (), s32[]{:S(2)}) async-start(), calls=%async_computation.13 | async-start | bytes 5308416 | tf_op jit(solution)/shard_map/all_gather | solution.py:326
  9.4 379.9 %all-gather.12.cloned.1.call-start = ((), (), s32[]{:S(2)}) async-start(), calls=%async_computation.14 | async-start | bytes 5308416 | tf_op jit(solution)/shard_map/all_gather | solution.py:327
  10.0 2132.2 %reduce-scatter.10.cloned.1.call-start = ((), (), s32[]{:S(2)}) async-start(), calls=%async_computation.15 | async-start | bytes 21233664 | tf_op jit(solution)/shard_map/reduce_scatter | solution.py:345
  16.7 289.7 %copy-start.9 = (s32[4096]{0:T(1024)}, s32[4096]{0:T(1024)S(1)}, u32[]{:S(2)}) copy-start(s32[4096]{0:T(1024)S(1)} %get-tuple-element.201) | copy-start | bytes 49156
  16.7 372.6 %copy-start.29 = (pred[4096]{0:T(1024)(128)(4,1)}, pred[4096]{0:T(1024)(128)(4,1)S(1)}, u32[]{:S(2)}) copy-start(pred[4096]{0:T(1024)(128)(4,1)S(1)} %compare_and_fusion) | copy-start | bytes 12292
  320.5 28.4 %copy-start.33 = (f32[4096]{0:T(1024)}, f32[4096]{0:T(1024)S(1)}, u32[]{:S(2)}) copy-start(f32[4096]{0:T(1024)S(1)} %get-tuple-element.343) | copy-start | bytes 49156
  1109.6 1035.8 %reduce-scatter.12.cloned.1.call-start = ((), (), s32[]{:S(2)}) async-start(), calls=%async_computation.16 | async-start | bytes 21233664 | tf_op jit(solution)/shard_map/reduce_scatter | solution.py:345
  1248.3 900.3 %reduce-scatter.14.cloned.1.call-start = ((), (), s32[]{:S(2)}) async-start(), calls=%async_computation.17 | async-start | bytes 21233664 | tf_op jit(solution)/shard_map/reduce_scatter | solution.py:345
  1387.4 764.5 %reduce-scatter.16.cloned.1.call-start = ((), (), s32[]{:S(2)}) async-start(), calls=%async_computation.18 | async-start | bytes 21233664 | tf_op jit(solution)/shard_map/reduce_scatter | solution.py:345
  1526.1 629.1 %reduce-scatter.18.cloned.1.call-start = ((), (), s32[]{:S(2)}) async-start(), calls=%async_computation.19 | async-start | bytes 21233664 | tf_op jit(solution)/shard_map/reduce_scatter | solution.py:345
  1664.8 493.6 %reduce-scatter.20.cloned.1.call-start = ((), (), s32[]{:S(2)}) async-start(), calls=%async_computation.20 | async-start | bytes 4866048 | tf_op jit(solution)/shard_map/reduce_scatter | solution.py:345
  1678.4 51.5 %copy-start.25 = (f32[768]{0:T(1024)S(1)}, f32[768]{0:T(1024)}, u32[]{:S(2)}) copy-start(f32[768]{0:T(1024)} %param.17) | copy-start | bytes 9220
  1739.0 30.8 %copy-start.20 = (f32[4096]{0:T(1024)}, f32[4096]{0:T(1024)S(1)}, u32[]{:S(2)}) copy-start(f32[4096]{0:T(1024)S(1)} %broadcast_multiply_fusion.2) | copy-start | bytes 49156
  1739.1 481.7 %reduce-scatter.26.cloned.1.call-start = ((), (), s32[]{:S(2)}) async-start(), calls=%async_computation.23 | async-start | bytes 10616832 | tf_op jit(solution)/shard_map/reduce_scatter | solution.py:352
  1769.4 451.4 %reduce-scatter.24.cloned.1.call-start = ((), (), s32[]{:S(2)}) async-start(), calls=%async_computation.22 | async-start | bytes 10616832 | tf_op jit(solution)/shard_map/reduce_scatter | solution.py:351
  1769.8 50.7 %copy-start.30 = (pred[4096]{0:T(1024)(128)(4,1)S(1)}, pred[4096]{0:T(1024)(128)(4,1)}, u32[]{:S(2)}) copy-start(pred[4096]{0:T(1024)(128)(4,1)} %copy-done.29) | copy-start | bytes 12292
  1769.8 50.7 %copy-start.34 = (f32[4096]{0:T(1024)S(1)}, f32[4096]{0:T(1024)}, u32[]{:S(2)}) copy-start(f32[4096]{0:T(1024)} %copy-done.33) | copy-start | bytes 49156
  1769.8 50.7 %copy-start.36 = (f32[768]{0:T(1024)S(1)}, f32[768]{0:T(1024)}, u32[]{:S(2)}) copy-start(f32[768]{0:T(1024)} %param.16) | copy-start | bytes 9220
  1847.8 42.8 %slice-start = ((s8[6291456]{0:T(1024)(128)(4,1)}), s8[2097152]{0:T(1024)(128)(4,1)S(1)}, s32[]{:S(2)}) async-start(s8[6291456]{0:T(1024)(128)(4,1)} %bitcast.138), calls=%async_computation.24 | async-start | bytes 4194304
  1847.9 373.0 %reduce-scatter.22.cloned.1.call-start = ((), (), s32[]{:S(2)}) async-start(), calls=%async_computation.21 | async-start | bytes 10616832 | tf_op jit(solution)/shard_map/reduce_scatter | solution.py:350
  1981.3 179.0 %all-to-all-start.1 = ((bf16[8,640,768]{2,1,0:T(8,128)(2,1)}), bf16[8,640,768]{2,1,0:T(8,128)(2,1)}, u32[]{:S(2)}, u32[]{:S(2)}) async-start(bf16[8,640,768]{2,1,0:T(8,128)(2,1)} %bitcast.140), calls=%async_computation.1 | async-start | bytes 15728640 | tf_op jit(solution)/shard_map/all_to_all | solution.py:358
  2002.4 139.8 %copy-start.31 = (s32[1,5120]{1,0:T(1,128)}, s32[1,5120]{1,0:T(1,128)S(1)}, u32[]{:S(2)}) copy-start(s32[1,5120]{1,0:T(1,128)S(1)} %constant_dynamic-update-slice_fusion.8.ids_ref) | copy-start | bytes 61444
  (27 other events, 508.9 us)
Sparse Core Ops, SparseCore 0:
  9.8 225.4 all-gather.5
  237.2 32.9 all-gather.7
  271.9 32.9 all-gather.9
  306.6 32.9 all-gather.11
  1109.7 117.1 reduce-scatter.9
  1248.4 117.1 reduce-scatter.11
  1387.5 117.1 reduce-scatter.13
  1526.2 117.1 reduce-scatter.15
  1665.0 117.1 reduce-scatter.17
  1785.4 43.2 reduce-scatter.19
  1832.6 67.4 reduce-scatter.25
  1904.0 67.4 reduce-scatter.23
  1975.4 137.4 reduce-scatter.21
